TPU v7x, 256 devices: a whole 4x4x8 slice. The times are simulated.
256 devices in a mesh: dp: 16 (over z, core), tensor: 16 (over y, x).
Axes of the slice: x: 4, y: 4, z: 8, core: 2. Of those that a mesh axis runs over, the one named last changes fastest.
Arguments:
- tokens: bfloat16 [4096, 4096], P('dp', 'tensor'), may hold values from -6 to 6
- cotangent: bfloat16 [4096, 4096], P('dp', 'tensor'), may hold values from -6 to 6
- gate_weight: bfloat16 [4096, 14336], P('dp', 'tensor'), may hold values from -0.09375 to 0.09375
- up_weight: bfloat16 [4096, 14336], P('dp', 'tensor'), may hold values from -0.09375 to 0.09375
- down_weight: bfloat16 [14336, 4096], P('tensor', 'dp'), may hold values from -0.046875 to 0.046875
- counts: int32 [16], replicated, may hold values from 0 to 16, as said below
Outputs:
- outputs: bfloat16 [4096, 4096], P('dp', 'tensor')
- input_grads: bfloat16 [4096, 4096], P('dp', 'tensor')
Inputs may be any that keep to these rules, and one draw needn't show every extreme that they name: counts[r] is the number of live 16-row blocks at the head of rank r's buffer; counts[r] + counts[(r + 8) % 16] = 16 for every rank r, some rank has 16 and some rank has 0.
All inputs are finite; a program needn't handle non-finite values.
Results may differ from a plain program's by a relative error of at most 0.005.
Values may be sent and summed in bfloat16 or wider, within the bound.
No kernel may reach another device: no remote copies, remote signals or barrier semaphores. Data moves between devices by JAX's collectives and lax.ppermute only.
A program may use at most 128 MiB of HBM per device.

v0:
```python
import jax
import jax.numpy as jnp
from jax import lax
from jax.sharding import PartitionSpec as P

BLOCK = 16


def side_by_side(arrays, axis, dim, along):
    both = jnp.concatenate(arrays, axis=along)
    result, at, finished = (lax.all_gather(both, axis, axis=dim, tiled=True), 0, [])
    for a in arrays:
        finished.append(lax.slice_in_dim(result, at, at + a.shape[along], axis=along))
        at += a.shape[along]
    return tuple(finished)


def in_one_piece(arrays, axis, dim, along):
    widths = [a.shape[along] for a in arrays]
    both = jnp.concatenate(arrays, axis=along)
    result = lax.psum_scatter(both, axis, scatter_dimension=dim, tiled=True)
    return tuple(jnp.split(result, [sum(widths[:k]) for k in range(1, len(widths))], axis=along))


def rows_first(arrays, axis, dims):
    turned = [jnp.moveaxis(a, dim, 0) for a, dim in zip(arrays, dims)]
    both = jnp.concatenate([t.reshape(len(t), -1) for t in turned], axis=1)
    result, at, finished = (lax.all_gather(both, axis, axis=0, tiled=True), 0, [])
    for t, dim in zip(turned, dims):
        piece = result[:, at : at + t[0].size].reshape(-1, *t.shape[1:])
        finished.append(jnp.moveaxis(piece, 0, dim))
        at += t[0].size
    return tuple(finished)


def passed_along(block, axis, distance):
    devices = range(lax.axis_size(axis))
    route = [((i - distance) % len(devices), i) for i in devices]
    return lax.ppermute(block, axis, route)


def transposed(left, right):
    return lax.dot_general(
        left, right, (((1,), (1,)), ((), ())), preferred_element_type=jnp.float32
    )


def mlp_rows(rows_x, rows_dy, live_rows, gate_full, up_full, down_full):
    whole_x, whole_dy = side_by_side((rows_x, rows_dy), "tensor", 1, 0)
    gate_pre = jnp.dot(whole_x, gate_full, preferred_element_type=jnp.float32)
    up_pre = jnp.dot(whole_x, up_full, preferred_element_type=jnp.float32)
    sigmoid_gate = jax.nn.sigmoid(gate_pre)
    activated = gate_pre * sigmoid_gate
    hidden = (activated * up_pre).astype(jnp.bfloat16)
    partial_y = jnp.dot(hidden, down_full, preferred_element_type=jnp.float32)
    grad_hidden = transposed(whole_dy, down_full)
    grad_gate = (
        grad_hidden * up_pre * sigmoid_gate * (1.0 + gate_pre * (1.0 - sigmoid_gate))
    ).astype(jnp.bfloat16)
    grad_up = (grad_hidden * activated).astype(jnp.bfloat16)
    partial_dx = transposed(grad_gate, gate_full) + transposed(grad_up, up_full)
    out_rows, grad_rows = in_one_piece((partial_y, partial_dx), "tensor", 1, 0)
    row_mask = live_rows[:, None]
    return ((out_rows * row_mask).astype(jnp.bfloat16), (grad_rows * row_mask).astype(jnp.bfloat16))


def per_device(tokens, cotangent, gate_weight, up_weight, down_weight, counts):
    gate_full, up_full, down_full = rows_first(
        (gate_weight, up_weight, down_weight), "dp", (0, 0, 1)
    )
    rank_count = lax.axis_size("dp")
    my_rank = lax.axis_index("dp")
    blocks = tokens.shape[0] // BLOCK
    columns = tokens.shape[1]
    own_blocks = counts[my_rank]
    share = blocks // 2
    half_ranks = rank_count // 2
    partner_count = counts[(my_rank + half_ranks) % rank_count]
    upper_x = tokens[share * BLOCK :]
    upper_dy = cotangent[share * BLOCK :]
    got_x, got_dy = passed_along((upper_x, upper_dy), "dp", half_ranks)
    keep_blocks = jnp.minimum(own_blocks, share)
    slot_ids = jnp.arange(share, dtype=jnp.int32)
    foreign = slot_ids - own_blocks
    mine = slot_ids < keep_blocks
    valid = mine | (foreign >= 0) & (foreign < partner_count - share)
    source_index = jnp.where(mine, slot_ids, share + jnp.clip(foreign, 0, share - 1))

    def assemble(lower, received):
        stacked = jnp.concatenate(
            [lower.reshape(share, BLOCK, columns), received.reshape(share, BLOCK, columns)], axis=0
        )
        pieces = jnp.take(stacked, source_index, axis=0)
        pieces = jnp.where(valid[:, None, None], pieces, jnp.zeros_like(pieces))
        return pieces.reshape(share * BLOCK, columns)

    work_x = assemble(tokens[: share * BLOCK], got_x)
    work_dy = assemble(cotangent[: share * BLOCK], got_dy)
    live_rows = jnp.repeat(valid.astype(jnp.float32), BLOCK)
    out_rows, grad_rows = mlp_rows(work_x, work_dy, live_rows, gate_full, up_full, down_full)
    back_pos = own_blocks + slot_ids
    back_ok = back_pos < share
    back_index = jnp.clip(back_pos, 0, share - 1)

    def send_back(source):
        pieces = jnp.take(source.reshape(share, BLOCK, columns), back_index, axis=0)
        pieces = jnp.where(back_ok[:, None, None], pieces, jnp.zeros_like(pieces))
        return pieces.reshape(share * BLOCK, columns)

    back_out, back_grad = passed_along(
        (send_back(out_rows), send_back(grad_rows)), "dp", half_ranks
    )
    upper_live = slot_ids < own_blocks - share

    def home_rows(worked, returned_rows):
        lower = jnp.where(
            mine[:, None, None],
            worked.reshape(share, BLOCK, columns),
            jnp.zeros((share, BLOCK, columns), worked.dtype),
        )
        upper = jnp.where(
            upper_live[:, None, None],
            returned_rows.reshape(share, BLOCK, columns),
            jnp.zeros((share, BLOCK, columns), worked.dtype),
        )
        return jnp.concatenate([lower, upper], axis=0).reshape(blocks * BLOCK, columns)

    outputs = home_rows(out_rows, back_out)
    input_grads = home_rows(grad_rows, back_grad)
    return (outputs, input_grads)


def solution(mesh):
    in_specs = (
        P("dp", "tensor"),
        P("dp", "tensor"),
        P("dp", "tensor"),
        P("dp", "tensor"),
        P("tensor", "dp"),
        P(),
    )
    out_specs = (P("dp", "tensor"), P("dp", "tensor"))
    return jax.shard_map(
        per_device, mesh=mesh, in_specs=in_specs, out_specs=out_specs, check_vma=False
    )
```

profile of v0, /device:TPU:2, one launch (start us, length us, event | category | flops | bytes accessed | tf_op | source)
XLA Modules:
  0.0 333.5 jit_solution(14445104334686321076)
XLA Ops:
  7.2 0.9 fusion.29
  8.1 7.3 %collective-permute-start = (bf16[128,256]{1,0:T(8,128)(2,1)S(1)}, bf16[128,256]{1,0:T(8,128)(2,1)S(1)}, u32[]{:S(2)}, u32[]{:S(2)}) collective-permute-start(bf16[128,256]{1,0:T(8,128)(2,1)S(1)} %get-tuple-element.11), channel_id=1, source_target_pairs={{128,0},{144,16},{160,32},{176,48},{192,64},{208,80},{224,96},{240... | collective-permute-start | bytes 196616 | tf_op jit(solution)/shard_map/ppermute | solution.py:39
  15.4 0.9 fusion.30
  16.4 1.3 fusion.31
  20.3 4.3 %collective-permute-done.1 = bf16[128,256]{1,0:T(8,128)(2,1)S(1)} collective-permute-done((bf16[128,256]{1,0:T(8,128)(2,1)S(1)}, bf16[128,256]{1,0:T(8,128)(2,1)S(1)}, u32[]{:S(2)}, u32[]{:S(2)}) %collective-permute-start.1) | collective-permute-done | bytes 65568 | tf_op jit(solution)/shard_map/ppermute | solution.py:39
  26.0 1.2 copy.8
  27.2 1.2 copy.9
  28.4 1.3 pad_maximum_fusion.1
  29.8 46.5 %all-gather.3.cloned.1.call-done = bf16[256,4096]{1,0:T(8,128)(2,1)} async-done(((bf16[256,256]{1,0:T(8,128)(2,1)}), bf16[256,4096]{1,0:T(8,128)(2,1)}) %all-gather.3.cloned.1.call-update) | async-done | bytes 2097168 | tf_op jit(solution)/shard_map/all_gather | solution.py:11
  76.3 128.1 %all-gather.5.cloned.1.call-done = bf16[4096,2688]{0,1:T(8,128)(2,1)} async-done(((bf16[256,2688]{0,1:T(8,128)(2,1)}), bf16[4096,2688]{0,1:T(8,128)(2,1)}) %all-gather.5.cloned.1.call-update) | async-done | bytes 22020112 | tf_op jit(solution)/shard_map/all_gather | solution.py:28
  204.4 6.0 %fusion.6 = f32[128,896]{1,0:T(8,128)S(1)} fusion(bf16[4096,2688]{0,1:T(8,128)(2,1)} %all-gather.5.cloned.1.call-done, bf16[256,4096]{1,0:T(8,128)(2,1)} %all-gather.3.cloned.1.call-done), kind=kOutput, calls=%fused_computation.10 | convolution fusion | flops 939524096 | bytes 8847360 | tf_op jit(solution)/shard_map/dot_general | solution.py:51
  210.4 6.6 %fusion.10 = f32[128,896]{1,0:T(8,128)S(1)} fusion(bf16[4096,2688]{0,1:T(8,128)(2,1)} %all-gather.5.cloned.1.call-done, bf16[256,4096]{1,0:T(8,128)(2,1)} %all-gather.3.cloned.1.call-done), kind=kOutput, calls=%fused_computation.14 | convolution fusion | flops 939524096 | bytes 8847360 | tf_op jit(solution)/shard_map/dot_general | solution.py:50
  217.0 3.8 %fusion = f32[128,896]{1,0:T(8,128)S(1)} fusion(bf16[4096,2688]{0,1:T(8,128)(2,1)S(1)} %copy-done.1, bf16[256,4096]{1,0:T(8,128)(2,1)} %all-gather.3.cloned.1.call-done), kind=kOutput, calls=%fused_computation.4 | convolution fusion | flops 939524096 | bytes 8847360 | tf_op jit(solution)/shard_map/dot_general | solution.py:43
  220.8 1.3 fusion.2
  222.1 1.3 fusion.4
  223.4 1.4 fusion.12
  224.8 2.4 pad_maximum_fusion
  229.4 79.4 %reduce-scatter.2.cloned.1.call-done = f32[256,256]{1,0:T(8,128)} async-done(((f32[256,4096]{1,0:T(8,128)}), f32[256,256]{1,0:T(8,128)}) %reduce-scatter.2.cloned.1.call-update) | async-done | bytes 262160 | tf_op jit(solution)/shard_map/reduce_scatter | solution.py:21
  308.8 1.0 fusion.20
  311.1 5.8 %collective-permute-start.2 = (bf16[128,256]{1,0:T(8,128)(2,1)S(1)}, bf16[128,256]{1,0:T(8,128)(2,1)S(1)}, u32[]{:S(2)}, u32[]{:S(2)}) collective-permute-start(bf16[128,256]{1,0:T(8,128)(2,1)S(1)} %bitcast.32), channel_id=1, source_target_pairs={{128,0},{144,16},{160,32},{176,48},{192,64},{208,80},{224,96},{240... | collective-permute-start | bytes 196616 | tf_op jit(solution)/shard_map/ppermute | solution.py:39
  317.2 3.0 collective-permute-done.2
  320.1 5.5 %collective-permute-done.3 = bf16[128,256]{1,0:T(8,128)(2,1)S(1)} collective-permute-done((bf16[128,256]{1,0:T(8,128)(2,1)S(1)}, bf16[128,256]{1,0:T(8,128)(2,1)S(1)}, u32[]{:S(2)}, u32[]{:S(2)}) %collective-permute-start.3) | collective-permute-done | bytes 65568 | tf_op jit(solution)/shard_map/ppermute | solution.py:39
  325.7 0.7 pad_maximum_fusion.6
  326.3 0.7 pad_maximum_fusion.5
  (33 shorter events, 5.9 us)
Async XLA Ops:
  7.2 21.3 %copy-start = (bf16[896,256]{1,0:T(8,128)(2,1)S(1)}, bf16[896,256]{1,0:T(8,128)(2,1)}, u32[]{:S(2)}) copy-start(bf16[896,256]{1,0:T(8,128)(2,1)} %param.14) | copy-start | bytes 1376260
  7.2 69.1 %all-gather.3.cloned.1.call-start = ((), (), s32[]{:S(2)}) async-start(), calls=%async_computation.1 | async-start | bytes 2228224 | tf_op jit(solution)/shard_map/all_gather | solution.py:11
  8.1 11.6 %collective-permute-start = (bf16[128,256]{1,0:T(8,128)(2,1)S(1)}, bf16[128,256]{1,0:T(8,128)(2,1)S(1)}, u32[]{:S(2)}, u32[]{:S(2)}) collective-permute-start(bf16[128,256]{1,0:T(8,128)(2,1)S(1)} %get-tuple-element.11), channel_id=1, source_target_pairs={{128,0},{144,16},{160,32},{176,48},{192,64},{208,80},{224,96},{240... | collective-permute-start | bytes 196616 | tf_op jit(solution)/shard_map/ppermute | solution.py:39
  16.3 8.3 %collective-permute-start.1 = (bf16[128,256]{1,0:T(8,128)(2,1)S(1)}, bf16[128,256]{1,0:T(8,128)(2,1)S(1)}, u32[]{:S(2)}, u32[]{:S(2)}) collective-permute-start(bf16[128,256]{1,0:T(8,128)(2,1)S(1)} %get-tuple-element.13), channel_id=1, source_target_pairs={{128,0},{144,16},{160,32},{176,48},{192,64},{208,80},{224,96},{240... | collective-permute-start | bytes 196616 | tf_op jit(solution)/shard_map/ppermute | solution.py:39
  25.9 178.5 %all-gather.5.cloned.1.call-start = ((), (), s32[]{:S(2)}) async-start(), calls=%async_computation.2 | async-start | bytes 23396352 | tf_op jit(solution)/shard_map/all_gather | solution.py:28
  29.8 279.0 %reduce-scatter.2.cloned.1.call-start = ((), (), s32[]{:S(2)}) async-start(), calls=%async_computation.3 | async-start | bytes 4456448 | tf_op jit(solution)/shard_map/reduce_scatter | solution.py:21
  204.4 12.6 %copy-start.1 = (bf16[4096,2688]{0,1:T(8,128)(2,1)S(1)}, bf16[4096,2688]{0,1:T(8,128)(2,1)}, u32[]{:S(2)}) copy-start(bf16[4096,2688]{0,1:T(8,128)(2,1)} %all-gather.5.cloned.1.call-done) | copy-start | bytes 66060292
  311.1 9.1 %collective-permute-start.2 = (bf16[128,256]{1,0:T(8,128)(2,1)S(1)}, bf16[128,256]{1,0:T(8,128)(2,1)S(1)}, u32[]{:S(2)}, u32[]{:S(2)}) collective-permute-start(bf16[128,256]{1,0:T(8,128)(2,1)S(1)} %bitcast.32), channel_id=1, source_target_pairs={{128,0},{144,16},{160,32},{176,48},{192,64},{208,80},{224,96},{240... | collective-permute-start | bytes 196616 | tf_op jit(solution)/shard_map/ppermute | solution.py:39
  316.9 8.7 %collective-permute-start.3 = (bf16[128,256]{1,0:T(8,128)(2,1)S(1)}, bf16[128,256]{1,0:T(8,128)(2,1)S(1)}, u32[]{:S(2)}, u32[]{:S(2)}) collective-permute-start(bf16[128,256]{1,0:T(8,128)(2,1)S(1)} %bitcast.30), channel_id=1, source_target_pairs={{128,0},{144,16},{160,32},{176,48},{192,64},{208,80},{224,96},{240... | collective-permute-start | bytes 196616 | tf_op jit(solution)/shard_map/ppermute | solution.py:39
Sparse Core Ops, SparseCore 0:
  26.1 50.1 all-gather.2
  78.0 126.3 all-gather.4
  227.4 81.3 reduce-scatter.1
where the time goes:
time: 334 us
  waiting for transfers between devices  267 us (80%)
  matrix products  20.3 us (6%)
  between operations  15.9 us (5%)
  starting transfers between devices  13.5 us (4%)
  other arithmetic  9.11 us (3%)
  local copies, waits for them, and re-layouts  7.94 us (2%)
    all_gather x1, waiting for transfers between devices, rows_first(): lax.all_gather(both, axis, axis=0, tiled=True)  128 us
    reduce_scatter x1, waiting for transfers between devices, in_one_piece(): result = lax.psum_scatter(both, axis, scatter_dimension=dim, tiled=True)  79.4 us
    all_gather x1, waiting for transfers between devices, side_by_side(): lax.all_gather(both, axis, axis=dim, tiled=True)  46.5 us
    ppermute x4, starting transfers between devices, passed_along(): return lax.ppermute(block, axis, route)  13.4 us
    ppermute x4, waiting for transfers between devices, passed_along(): return lax.ppermute(block, axis, route)  12.7 us
  transfers between devices with their start and end apart: 7, of which 6 were waited for; matrix products, arithmetic and copies ran while one was open for 3% of the time, Pallas kernels for 0%

commit v1 on v0

v1 whole, which is shorter than its diff:
```python
import math

import jax
import jax.numpy as jnp
from jax import lax
from jax.experimental import pallas as pl
from jax.experimental.pallas import tpu as pltpu
from jax.sharding import PartitionSpec as P


BLOCK = 16
SIDE = 4
RING = 8
FAR = 4
TILE = 256
NEAR = (0, 7, 1, 6, 2, 5, 3)
F32 = jnp.float32
BF16 = jnp.bfloat16


def ring(block, step):
    route = [(((d // 2 - step) % RING) * 2 + d % 2, d) for d in range(2 * RING)]
    return lax.ppermute(block, "dp", route)


def swap(block):
    return lax.ppermute(block, "dp", [(d, d ^ 1) for d in range(2 * RING)])


def opposite(block):
    n = 2 * RING
    return lax.ppermute(block, "dp", [((d + n // 2) % n, d) for d in range(n)])


def dot(left, right):
    return jnp.dot(left, right, preferred_element_type=F32)


def size(shape, dtype):
    return math.prod(shape) * jnp.dtype(dtype).itemsize


def call(body, outs, scalars, *arrays):
    specs = [pl.BlockSpec(memory_space=pltpu.SMEM)]
    specs += [pl.BlockSpec(memory_space=pltpu.VMEM)] * len(arrays)
    held = sum(size(a.shape, a.dtype) for a in arrays) + sum(size(*o) for o in outs)
    return pl.pallas_call(
        body,
        out_shape=[jax.ShapeDtypeStruct(s, d) for s, d in outs],
        in_specs=specs,
        out_specs=[pl.BlockSpec(memory_space=pltpu.VMEM)] * len(outs),
        compiler_params=pltpu.CompilerParams(vmem_limit_bytes=held + (4 << 20)),
    )(scalars, *arrays)


CORE, SLOT, CHIP = 0, 1, 1 + RING


def arrange_features(table, mine, other, x_out, dy_out):
    rows = mine.shape[3]
    for core in range(2):

        @pl.when(table[CORE] == core)
        def _():
            at, away = core * rows, (1 - core) * rows
            for k in range(RING):
                slot = table[SLOT + k]
                for which, out in ((0, x_out), (1, dy_out)):
                    out[k, :, at : at + rows] = mine[slot, which]
                    out[k, :, away : away + rows] = other[slot, which]


def tiles(extent, size):
    return [(at, min(at + size, extent)) for at in range(0, extent, size)]


def gate_up_kernel(table, x, *refs):
    gates, ups, out = refs[:RING], refs[RING : 2 * RING], refs[2 * RING]
    for which, weights in ((0, gates), (1, ups)):
        for lo, hi in tiles(out.shape[1], TILE):
            out[which, lo:hi] = sum(dot(weights[k][lo:hi], x[k]) for k in range(RING))


def grad_hidden_kernel(table, dy, *refs):
    downs, out = refs[:-1], refs[-1]
    for lo, hi in tiles(out.shape[0], TILE):
        out[lo:hi] = sum(dot(downs[n][lo:hi], dy[k]) for n, k in enumerate(NEAR))


def grad_hidden_far(table, dy, near, far_a, far_b, out):
    cut = far_a.shape[0]
    out[:cut] = near[:cut] + dot(far_a[...], dy[FAR])
    out[cut:] = near[cut:] + dot(far_b[...], dy[FAR])


def keep_and_give(table, k, block, keep, give):
    rows = keep.shape[1]

    @pl.when(table[CORE] == 0)
    def _():
        keep[k] = block[:rows]
        give[k] = block[rows:]

    @pl.when(table[CORE] != 0)
    def _():
        keep[k] = block[rows:]
        give[k] = block[:rows]


def outputs_kernel(table, hidden_t, far_a, far_b, *refs):
    downs, (keep, give, hidden) = refs[:-3], refs[-3:]
    cut = far_a.shape[0]
    hidden[...] = hidden_t[...].T
    for n, k in enumerate(NEAR):
        keep_and_give(table, k, dot(hidden[...], downs[n][...]).astype(BF16), keep, give)
    far = dot(hidden[:, :cut], far_a[...]) + dot(hidden[:, cut:], far_b[...])
    keep_and_give(table, FAR, far.astype(BF16), keep, give)


def input_grads_kernel(table, mine, other, by_gate, by_up, *refs):
    gates, ups = refs[:RING], refs[RING : 2 * RING]
    keep, give, gg, gu = refs[2 * RING :]
    for lo, hi in tiles(mine.shape[0], TILE):
        grad_hidden = mine[lo:hi] + other[lo:hi]
        gg[:, lo:hi] = (grad_hidden * by_gate[lo:hi]).astype(BF16).T
        gu[:, lo:hi] = (grad_hidden * by_up[lo:hi]).astype(BF16).T
    for k in range(RING):
        block = dot(gg[...], gates[k][...]) + dot(gu[...], ups[k][...])
        keep_and_give(table, k, block.astype(BF16), keep, give)


def arrange_columns(table, mine, other, out):
    for s in range(2 * RING):
        k = (s // 2 - table[CHIP] + RING) % RING

        @pl.when(table[CORE] == s % 2)
        def _():
            out[s] = mine[k]

        @pl.when(table[CORE] != s % 2)
        def _():
            out[s] = other[k]


def per_device(tokens, cotangent, gate_weight, up_weight, down_weight, counts):
    rank = lax.axis_index("dp")
    z, c = rank // 2, rank % 2

    def around(own, after=None):
        right, left = [own], [own]
        for n in range(3):
            next_r, next_l = right[-1], left[-1]
            if n == 1 and after:
                next_r, _ = lax.optimization_barrier((next_r, after[0]))
                next_l, _ = lax.optimization_barrier((next_l, after[1]))
            right.append(ring(next_r, 1))
            left.append(ring(next_l, -1))
        return right, left

    g_r, g_l = around(gate_weight.T)
    u_r, u_l = around(up_weight.T)
    g_far, u_far = ring(g_r[3], 1), ring(u_l[3], -1)
    d_r, d_l = around(down_weight, (g_r[3], g_l[3]))
    cut = 512
    d_far = (ring(d_r[3][:cut], 1), ring(d_l[3][cut:], -1))

    def by_delta(r, l, far):
        return [r[0], l[1], l[2], l[3], far, r[3], r[2], r[1]]

    gates = by_delta(g_r, g_l, g_far)
    ups = by_delta(u_r, u_l, u_far)
    downs = by_delta(d_r, d_l, None)
    near_downs = [downs[k] for k in NEAR]

    rank_count = lax.axis_size("dp")
    blocks = tokens.shape[0] // BLOCK
    columns = tokens.shape[1]
    own_blocks = counts[rank]
    share = blocks // 2
    rows = share * BLOCK
    partner_count = counts[(rank + rank_count // 2) % rank_count]
    got = opposite(jnp.stack([tokens[rows:], cotangent[rows:]]))
    keep_blocks = jnp.minimum(own_blocks, share)
    slot_ids = jnp.arange(share, dtype=jnp.int32)
    foreign = slot_ids - own_blocks
    mine = slot_ids < keep_blocks
    valid = mine | (foreign >= 0) & (foreign < partner_count - share)
    source_index = jnp.where(mine, slot_ids, share + jnp.clip(foreign, 0, share - 1))
    lower = jnp.stack([tokens[:rows], cotangent[:rows]])
    stacked = jnp.concatenate([lower.reshape(2, share, BLOCK, columns), got.reshape(2, share, BLOCK, columns)], axis=1)
    pieces = jnp.take(stacked, source_index, axis=1)
    pieces = jnp.where(valid[None, :, None, None], pieces, jnp.zeros_like(pieces))
    work = pieces.reshape(2, rows, columns).transpose(0, 2, 1)
    live_rows = jnp.repeat(valid.astype(F32), BLOCK)[:, None]

    spread = jnp.broadcast_to(work[None], (SIDE * SIDE, *work.shape))
    every = lax.all_to_all(spread, "tensor", 0, 0, tiled=True)
    slots = 2 * ((z + jnp.arange(RING, dtype=jnp.int32)) % RING) + c
    every_other = swap(every)
    table = jnp.concatenate([c[None], slots, z[None]]).astype(jnp.int32)
    wide = (RING, columns, 2 * rows)
    x_all, dy_all = call(arrange_features, [(wide, BF16)] * 2, table, every, every_other)

    ff = gate_weight.shape[1]
    by_row = (ff, 2 * rows)
    turned = ((2 * rows, ff), BF16)
    parts = call(gate_up_kernel, [((2,) + by_row, F32)], table, x_all, *gates, *ups)[0]
    sums = parts + swap(parts)
    gate_pre, up_pre = sums[0], sums[1]
    sigmoid_gate = jax.nn.sigmoid(gate_pre)
    activated = gate_pre * sigmoid_gate
    hidden = (activated * up_pre).astype(BF16)
    by_gate = up_pre * sigmoid_gate * (1.0 + gate_pre * (1.0 - sigmoid_gate))

    half = ((RING, rows, columns), BF16)

    def reduce_columns(keep, give):
        share_of = ((2 * RING, rows, columns), BF16)
        blocks_for = call(arrange_columns, [share_of], table, keep, swap(give))[0]
        got_blocks = lax.all_to_all(blocks_for, "tensor", 0, 0, tiled=True)
        return jnp.sum(got_blocks.astype(F32), axis=0)

    grad_near = call(grad_hidden_kernel, [(by_row, F32)], table, dy_all, *near_downs)[0]
    grad_part = call(grad_hidden_far, [(by_row, F32)], table, dy_all, grad_near, *d_far)[0]
    grad_other = swap(grad_part)
    out = call(outputs_kernel, [half, half, turned], table, hidden, *d_far, *near_downs)
    out_sum = reduce_columns(out[0], out[1])
    dx = call(input_grads_kernel, [half, half, turned, turned], table, grad_part, grad_other, by_gate, activated, *gates, *ups)
    dx_sum = reduce_columns(dx[0], dx[1])

    back_pos = own_blocks + slot_ids
    back_ok = back_pos < share
    back_index = jnp.clip(back_pos, 0, share - 1)
    upper_live = slot_ids < own_blocks - share

    done = (jnp.stack([out_sum, dx_sum]) * live_rows).astype(BF16).reshape(2, share, BLOCK, columns)
    back = jnp.take(done, back_index, axis=1)
    back = jnp.where(back_ok[:, None, None], back, jnp.zeros_like(back))
    returned = opposite(back)
    low = jnp.where(mine[:, None, None], done, jnp.zeros_like(done))
    high = jnp.where(upper_live[:, None, None], returned, jnp.zeros_like(returned))
    home = jnp.concatenate([low, high], axis=1).reshape(2, 2 * rows, columns)
    return home[0], home[1]


def solution(mesh):
    in_specs = (
        P("dp", "tensor"),
        P("dp", "tensor"),
        P("dp", "tensor"),
        P("dp", "tensor"),
        P("tensor", "dp"),
        P(),
    )
    out_specs = (P("dp", "tensor"), P("dp", "tensor"))

    return jax.shard_map(per_device, mesh=mesh, in_specs=in_specs, out_specs=out_specs, check_vma=False)
```

time: 334 us -> 249 us (0.75)
  waiting for transfers between devices: 267 us -> 98 us
  starting transfers between devices: 13.5 us -> 63.4 us
  blocking collectives: 0 us -> 34.1 us
  Pallas kernels: 0 us -> 25.9 us
  matrix products: 20.3 us -> 0 us
  between operations: 15.9 us -> 2.93 us
  local copies, waits for them, and re-layouts: 7.94 us -> 16 us
    all_gather x2 -> x0, waiting for transfers between devices: 175 us -> none  [the longest x1 128 us: rows_first(): lax.all_gather(both, axis, axis=0, tiled=True)]
    reduce_scatter x1 -> x0, waiting for transfers between devices: 79.4 us -> none  [in_one_piece(): result = lax.psum_scatter(both, axis, scatter_dimension=dim, tiled=True)]
    ppermute x4 -> x29, waiting for transfers between devices: 12.7 us -> 84 us  [the longest x22 75.5 us: ring(): return lax.ppermute(block, 'dp', route)]
    ppermute x4 -> x29, starting transfers between devices: 13.4 us -> 50.6 us  [the longest x22 38.9 us: ring(): return lax.ppermute(block, 'dp', route)]
    all_to_all x0 -> x1, blocking collectives: none -> 34.1 us  [per_device(): every = lax.all_to_all(spread, 'tensor', 0, 0, tiled=True)]
    pallas_call x0 -> x8, Pallas kernels: none -> 25.9 us  [call(): pl.pallas_call(body, out_shape=[jax.ShapeDtypeStruct(s, d) for s, d in ou...]
    dot_general x6 -> x0, matrix products: 20.3 us -> none  [the longest x1 6.59 us: mlp_rows(): gate_pre = jnp.dot(whole_x, gate_full, preferred_element_type=jnp.float32)]
    all_to_all x0 -> x2, waiting for transfers between devices: none -> 14 us  [reduce_columns(): got_blocks = lax.all_to_all(blocks_for, 'tensor', 0, 0, tiled=True)]
  transfers between devices with their start and end apart: 7 -> 31, of which waited for: 6 -> 19; matrix products, arithmetic and copies ran while one was open for 3% -> 4% of each run, Pallas kernels for 0% -> 7%
where the time goes in v1:
time: 249 us; the launch traced here: 248 us
  waiting for transfers between devices  98 us (39%)
  starting transfers between devices  63.4 us (25%)
  blocking collectives  34.1 us (14%)
  Pallas kernels  25.9 us (10%)
  local copies, waits for them, and re-layouts  16 us (6%)
  other arithmetic  7.34 us (3%)
  between operations  2.93 us (1%)
    ppermute x22, waiting for transfers between devices, ring(): return lax.ppermute(block, 'dp', route)  75.5 us
    ppermute x22, starting transfers between devices, ring(): return lax.ppermute(block, 'dp', route)  38.9 us
    all_to_all x1, blocking collectives, per_device(): every = lax.all_to_all(spread, 'tensor', 0, 0, tiled=True)  34.1 us
    pallas_call x8, Pallas kernels, call(): pl.pallas_call(body, out_shape=[jax.ShapeDtypeStruct(s, d) for s, d in ou...  25.9 us
    all_to_all x2, waiting for transfers between devices, reduce_columns(): got_blocks = lax.all_to_all(blocks_for, 'tensor', 0, 0, tiled=True)  14 us
    all_to_all x2, starting transfers between devices, reduce_columns(): got_blocks = lax.all_to_all(blocks_for, 'tensor', 0, 0, tiled=True)  12.8 us
    unnamed x40, local copies, waits for them, and re-layouts  11.6 us
    ppermute x2, starting transfers between devices, opposite(): return lax.ppermute(block, 'dp', [((d + n // 2) % n, d) for d in range(n)])  10.9 us
  transfers between devices with their start and end apart: 31, of which 19 were waited for; matrix products, arithmetic and copies ran while one was open for 4% of the time, Pallas kernels for 7%

profile of v1, /device:TPU:2, one launch (start us, length us, event | category | flops | bytes accessed | tf_op | source)
XLA Modules:
  0.0 247.7 jit_solution(8549648292688606415)
XLA Ops:
  1.6 7.3 %collective-permute-start = (bf16[2,128,256]{2,1,0:T(8,128)(2,1)S(1)}, bf16[2,128,256]{2,1,0:T(8,128)(2,1)S(1)}, u32[]{:S(2)}, u32[]{:S(2)}) collective-permute-start(bf16[2,128,256]{2,1,0:T(8,128)(2,1)S(1)} %pad_maximum_fusion.2), channel_id=1, source_target_pairs={{128,0},{144,16},{160,32},{176,48},{192,64},{208,80},{224,96},{240... | collective-permute-start | bytes 393224 | tf_op jit(solution)/shard_map/ppermute | solution.py:32
  15.2 34.1 %all_to_all.15.mine = bf16[16,2,256,128]{3,2,1,0:T(8,128)(2,1)S(1)} all-to-all(bf16[16,2,256,128]{3,2,1,0:T(8,128)(2,1)S(1)} %broadcast_in_dim.81), channel_id=1, replica_groups=mesh['dp'=16,'tensor'=16] {'tensor'}, dimensions={0} | all-to-all | bytes 4194304 | tf_op jit(solution)/shard_map/all_to_all | solution.py:197
  57.3 7.9 %collective-permute-done.5.refs_7_ = bf16[896,256]{1,0:T(8,128)(2,1)S(1)} collective-permute-done((bf16[896,256]{1,0:T(8,128)(2,1)S(1)}, bf16[896,256]{1,0:T(8,128)(2,1)S(1)}, u32[]{:S(2)}, u32[]{:S(2)}) %collective-permute-start.5) | collective-permute-done | bytes 458784 | tf_op jit(solution)/shard_map/ppermute | solution.py:23
  66.1 3.7 %collective-permute-start.10 = (bf16[896,256]{1,0:T(8,128)(2,1)S(1)}, bf16[896,256]{1,0:T(8,128)(2,1)S(1)}, u32[]{:S(2)}, u32[]{:S(2)}) collective-permute-start(bf16[896,256]{1,0:T(8,128)(2,1)S(1)} %collective-permute-done.9.refs_9_), channel_id=1, source_target_pairs={{32,0},{48,16},{64,32},{80,48},{96,64},{112,80},{128,96},{144,112}... | collective-permute-start | bytes 1376264 | tf_op jit(solution)/shard_map/ppermute | solution.py:23
  70.6 5.4 %collective-permute-done.2.refs_1_ = bf16[896,256]{1,0:T(8,128)(2,1)S(1)} collective-permute-done((bf16[896,256]{1,0:T(8,128)(2,1)S(1)}, bf16[896,256]{1,0:T(8,128)(2,1)S(1)}, u32[]{:S(2)}, u32[]{:S(2)}) %collective-permute-start.2) | collective-permute-done | bytes 458784 | tf_op jit(solution)/shard_map/ppermute | solution.py:23
  75.9 3.7 %collective-permute-start.3 = (bf16[896,256]{1,0:T(8,128)(2,1)S(1)}, bf16[896,256]{1,0:T(8,128)(2,1)}, u32[]{:S(2)}, u32[]{:S(2)}) collective-permute-start(bf16[896,256]{1,0:T(8,128)(2,1)S(1)} %collective-permute-done.2.refs_1_), channel_id=1, source_target_pairs={{32,0},{48,16},{64,32},{80,48},{96,64},{112,80},{128,96},{144,112}... | collective-permute-start | bytes 1376264 | tf_op jit(solution)/shard_map/ppermute | solution.py:23
  81.2 3.7 %collective-permute-done.6.refs_6_ = bf16[896,256]{1,0:T(8,128)(2,1)S(1)} collective-permute-done((bf16[896,256]{1,0:T(8,128)(2,1)S(1)}, bf16[896,256]{1,0:T(8,128)(2,1)S(1)}, u32[]{:S(2)}, u32[]{:S(2)}) %collective-permute-start.6) | collective-permute-done | bytes 458784 | tf_op jit(solution)/shard_map/ppermute | solution.py:23
  85.8 3.7 %collective-permute-start.11 = (bf16[896,256]{1,0:T(8,128)(2,1)S(1)}, bf16[896,256]{1,0:T(8,128)(2,1)}, u32[]{:S(2)}, u32[]{:S(2)}) collective-permute-start(bf16[896,256]{1,0:T(8,128)(2,1)S(1)} %collective-permute-done.10.refs_10_), channel_id=1, source_target_pairs={{32,0},{48,16},{64,32},{80,48},{96,64},{112,80},{128,96},{144,112}... | collective-permute-start | bytes 1376264 | tf_op jit(solution)/shard_map/ppermute | solution.py:23
  90.2 5.4 %collective-permute-done.3.refs_2_ = bf16[896,256]{1,0:T(8,128)(2,1)} collective-permute-done((bf16[896,256]{1,0:T(8,128)(2,1)S(1)}, bf16[896,256]{1,0:T(8,128)(2,1)}, u32[]{:S(2)}, u32[]{:S(2)}) %collective-permute-start.3) | collective-permute-done | bytes 458784 | tf_op jit(solution)/shard_map/ppermute | solution.py:23
  95.6 3.8 %collective-permute-start.4 = (bf16[896,256]{1,0:T(8,128)(2,1)}, bf16[896,256]{1,0:T(8,128)(2,1)}, u32[]{:S(2)}, u32[]{:S(2)}) collective-permute-start(bf16[896,256]{1,0:T(8,128)(2,1)} %collective-permute-done.3.refs_2_), channel_id=1, source_target_pairs={{32,0},{48,16},{64,32},{80,48},{96,64},{112,80},{128,96},{144,112}... | collective-permute-start | bytes 1376264 | tf_op jit(solution)/shard_map/ppermute | solution.py:23
  99.4 5.5 %collective-permute-done.7.refs_5_ = bf16[896,256]{1,0:T(8,128)(2,1)} collective-permute-done((bf16[896,256]{1,0:T(8,128)(2,1)S(1)}, bf16[896,256]{1,0:T(8,128)(2,1)}, u32[]{:S(2)}, u32[]{:S(2)}) %collective-permute-start.7) | collective-permute-done | bytes 458784 | tf_op jit(solution)/shard_map/ppermute | solution.py:23
  105.4 3.8 %collective-permute-start.12 = (bf16[896,256]{1,0:T(8,128)(2,1)}, bf16[896,256]{1,0:T(8,128)(2,1)}, u32[]{:S(2)}, u32[]{:S(2)}) collective-permute-start(bf16[896,256]{1,0:T(8,128)(2,1)} %collective-permute-done.11.refs_11_), channel_id=1, source_target_pairs={{32,0},{48,16},{64,32},{80,48},{96,64},{112,80},{128,96},{144,112}... | collective-permute-start | bytes 1376264 | tf_op jit(solution)/shard_map/ppermute | solution.py:23
  111.5 3.9 %collective-permute-done.4.refs_3_ = bf16[896,256]{1,0:T(8,128)(2,1)} collective-permute-done((bf16[896,256]{1,0:T(8,128)(2,1)}, bf16[896,256]{1,0:T(8,128)(2,1)}, u32[]{:S(2)}, u32[]{:S(2)}) %collective-permute-start.4) | collective-permute-done | bytes 458784 | tf_op jit(solution)/shard_map/ppermute | solution.py:23
  115.4 8.8 %collective-permute-done.8.refs_4_ = bf16[896,256]{1,0:T(8,128)(2,1)} collective-permute-done((bf16[896,256]{1,0:T(8,128)(2,1)}, bf16[896,256]{1,0:T(8,128)(2,1)}, u32[]{:S(2)}, u32[]{:S(2)}) %collective-permute-start.8) | collective-permute-done | bytes 458784 | tf_op jit(solution)/shard_map/ppermute | solution.py:23
  124.8 4.1 %shard_map.78 = f32[2,896,256]{2,1,0:T(8,128)S(1)} custom-call(s32[10]{0:T(128)S(1)} %pad_add_fusion.table, bf16[8,256,256]{2,1,0:T(8,128)(2,1)S(1)} %get-tuple-element.10.x, bf16[896,256]{1,0:T(8,128)(2,1)S(1)} %bitcast.45, bf16[896,256]{1,0:T(8,128)(2,1)S(1)} %copy-done.7, bf16[896,256]{1,0:T(8,128)(2,1)} %collective-permute-done.3.refs_2_, ...), custom_call_target="tpu_custom_call" | custom-call | tf_op jit(solution)/shard_map/pallas_call | solution.py:47
  132.9 11.0 %collective-permute-done.17.refs_1_ = bf16[896,256]{1,0:T(8,128)(2,1)S(1)} collective-permute-done((bf16[896,256]{1,0:T(8,128)(2,1)S(1)}, bf16[896,256]{1,0:T(8,128)(2,1)S(1)}, u32[]{:S(2)}, u32[]{:S(2)}) %collective-permute-start.17) | collective-permute-done | bytes 458784 | tf_op jit(solution)/shard_map/ppermute | solution.py:23
  147.1 10.2 %collective-permute-done.18.refs_3_ = bf16[896,256]{1,0:T(8,128)(2,1)S(1)} collective-permute-done((bf16[896,256]{1,0:T(8,128)(2,1)S(1)}, bf16[896,256]{1,0:T(8,128)(2,1)S(1)}, u32[]{:S(2)}, u32[]{:S(2)}) %collective-permute-start.18) | collective-permute-done | bytes 458784 | tf_op jit(solution)/shard_map/ppermute | solution.py:23
  160.6 9.4 %collective-permute-done.19.refs_5_ = bf16[896,256]{1,0:T(8,128)(2,1)S(1)} collective-permute-done((bf16[896,256]{1,0:T(8,128)(2,1)S(1)}, bf16[896,256]{1,0:T(8,128)(2,1)S(1)}, u32[]{:S(2)}, u32[]{:S(2)}) %collective-permute-start.19) | collective-permute-done | bytes 458784 | tf_op jit(solution)/shard_map/ppermute | solution.py:23
  177.6 4.8 %shard_map.79 = (bf16[8,128,256]{2,1,0:T(8,128)(2,1)S(1)}, bf16[8,128,256]{2,1,0:T(8,128)(2,1)S(1)}, bf16[256,896]{1,0:T(8,128)(2,1)}) custom-call(s32[10]{0:T(128)S(1)} %pad_add_fusion.table, bf16[896,256]{1,0:T(8,128)(2,1)S(1)} %get-tuple-element.22.hidden_t, bf16[512,256]{1,0:T(8,128)(2,1)S(1)} %collective-permute-done.20.far_a, ...), custom_call_target="tpu_custom_call" | custom-call | tf_op jit(solution)/shard_map/pallas_call | solution.py:47
  187.3 5.5 %all-to-all-start.1 = ((bf16[16,128,256]{2,1,0:T(8,128)(2,1)}), bf16[16,128,256]{2,1,0:T(8,128)(2,1)}, u32[]{:S(2)}, u32[]{:S(2)}) async-start(bf16[16,128,256]{2,1,0:T(8,128)(2,1)} %shard_map.80), calls=%async_computation.1 | async-start | bytes 2097152 | tf_op jit(solution)/shard_map/all_to_all | solution.py:220
  199.1 8.8 %shard_map.83 = (bf16[8,128,256]{2,1,0:T(8,128)(2,1)S(1)}, bf16[8,128,256]{2,1,0:T(8,128)(2,1)S(1)}, bf16[256,896]{1,0:T(8,128)(2,1)}, bf16[256,896]{1,0:T(8,128)(2,1)}) custom-call(s32[10]{0:T(128)S(1)} %pad_add_fusion.table, f32[896,256]{1,0:T(8,128)S(1)} %shard_map.82.mine, f32[896,256]{1,0:T(8,128)} %collective-permute-done.26.other, ...), custom_call_target="tpu_custom_call" | custom-call | tf_op jit(solution)/shard_map/pallas_call | solution.py:47
  211.7 7.3 %all-to-all-start.2 = ((bf16[16,128,256]{2,1,0:T(8,128)(2,1)}), bf16[16,128,256]{2,1,0:T(8,128)(2,1)S(1)}, u32[]{:S(2)}, u32[]{:S(2)}) async-start(bf16[16,128,256]{2,1,0:T(8,128)(2,1)} %shard_map.84), calls=%async_computation.2 | async-start | bytes 2097152 | tf_op jit(solution)/shard_map/all_to_all | solution.py:220
  221.0 14.0 %all-to-all-done.2 = bf16[16,128,256]{2,1,0:T(8,128)(2,1)S(1)} async-done(((bf16[16,128,256]{2,1,0:T(8,128)(2,1)}), bf16[16,128,256]{2,1,0:T(8,128)(2,1)S(1)}, u32[]{:S(2)}, u32[]{:S(2)}) %all-to-all-start.2) | async-done | bytes 1048608 | tf_op jit(solution)/shard_map/all_to_all | solution.py:220
  240.3 6.6 %collective-permute-done.28 = bf16[2,8,16,256]{3,2,0,1:T(8,128)(2,1)S(1)} collective-permute-done((bf16[2,8,16,256]{3,2,0,1:T(8,128)(2,1)S(1)}, bf16[2,8,16,256]{3,2,0,1:T(8,128)(2,1)S(1)}, u32[]{:S(2)}, u32[]{:S(2)}) %collective-permute-start.28) | collective-permute-done | bytes 131104 | tf_op jit(solution)/shard_map/ppermute | solution.py:32
  (121 shorter events, 62.3 us)
Async XLA Ops:
  49.3 60.0 %collective-permute-start.1 = (bf16[16,2,256,128]{3,2,1,0:T(8,128)(2,1)S(1)}, bf16[16,2,256,128]{3,2,1,0:T(8,128)(2,1)}, u32[]{:S(2)}, u32[]{:S(2)}) collective-permute-start(bf16[16,2,256,128]{3,2,1,0:T(8,128)(2,1)S(1)} %all_to_all.15.mine), channel_id=1, source_target_pairs={{0,16},{16,0},{32,48},{48,32},{64,80},{80,64},{96,112},{112,96},{1... | collective-permute-start | bytes 6291464 | tf_op jit(solution)/shard_map/ppermute | solution.py:27
  49.5 15.7 %collective-permute-start.5 = (bf16[896,256]{1,0:T(8,128)(2,1)S(1)}, bf16[896,256]{1,0:T(8,128)(2,1)S(1)}, u32[]{:S(2)}, u32[]{:S(2)}) collective-permute-start(bf16[896,256]{1,0:T(8,128)(2,1)S(1)} %bitcast.43), channel_id=1, source_target_pairs={{224,0},{240,16},{0,32},{16,48},{32,64},{48,80},{64,96},{80,112},{... | collective-permute-start | bytes 1376264 | tf_op jit(solution)/shard_map/ppermute | solution.py:23
  52.3 13.8 %collective-permute-start.9 = (bf16[896,256]{1,0:T(8,128)(2,1)S(1)}, bf16[896,256]{1,0:T(8,128)(2,1)S(1)}, u32[]{:S(2)}, u32[]{:S(2)}) collective-permute-start(bf16[896,256]{1,0:T(8,128)(2,1)S(1)} %bitcast.47), channel_id=1, source_target_pairs={{32,0},{48,16},{64,32},{80,48},{96,64},{112,80},{128,96},{144,112}... | collective-permute-start | bytes 1376264 | tf_op jit(solution)/shard_map/ppermute | solution.py:23
  55.2 20.7 %collective-permute-start.2 = (bf16[896,256]{1,0:T(8,128)(2,1)S(1)}, bf16[896,256]{1,0:T(8,128)(2,1)S(1)}, u32[]{:S(2)}, u32[]{:S(2)}) collective-permute-start(bf16[896,256]{1,0:T(8,128)(2,1)S(1)} %bitcast.44), channel_id=1, source_target_pairs={{32,0},{48,16},{64,32},{80,48},{96,64},{112,80},{128,96},{144,112}... | collective-permute-start | bytes 1376264 | tf_op jit(solution)/shard_map/ppermute | solution.py:23
  57.3 23.1 %collective-permute-start.13 = (bf16[896,256]{1,0:T(8,128)(2,1)S(1)}, bf16[896,256]{1,0:T(8,128)(2,1)S(1)}, u32[]{:S(2)}, u32[]{:S(2)}) collective-permute-start(bf16[896,256]{1,0:T(8,128)(2,1)S(1)} %bitcast.48), channel_id=1, source_target_pairs={{224,0},{240,16},{0,32},{16,48},{32,64},{48,80},{64,96},{80,112},{... | collective-permute-start | bytes 1376264 | tf_op jit(solution)/shard_map/ppermute | solution.py:23
  65.2 19.7 %collective-permute-start.6 = (bf16[896,256]{1,0:T(8,128)(2,1)S(1)}, bf16[896,256]{1,0:T(8,128)(2,1)S(1)}, u32[]{:S(2)}, u32[]{:S(2)}) collective-permute-start(bf16[896,256]{1,0:T(8,128)(2,1)S(1)} %collective-permute-done.5.refs_7_), channel_id=1, source_target_pairs={{224,0},{240,16},{0,32},{16,48},{32,64},{48,80},{64,96},{80,112},{... | collective-permute-start | bytes 1376264 | tf_op jit(solution)/shard_map/ppermute | solution.py:23
  66.1 19.7 %collective-permute-start.10 = (bf16[896,256]{1,0:T(8,128)(2,1)S(1)}, bf16[896,256]{1,0:T(8,128)(2,1)S(1)}, u32[]{:S(2)}, u32[]{:S(2)}) collective-permute-start(bf16[896,256]{1,0:T(8,128)(2,1)S(1)} %collective-permute-done.9.refs_9_), channel_id=1, source_target_pairs={{32,0},{48,16},{64,32},{80,48},{96,64},{112,80},{128,96},{144,112}... | collective-permute-start | bytes 1376264 | tf_op jit(solution)/shard_map/ppermute | solution.py:23
  75.9 19.7 %collective-permute-start.3 = (bf16[896,256]{1,0:T(8,128)(2,1)S(1)}, bf16[896,256]{1,0:T(8,128)(2,1)}, u32[]{:S(2)}, u32[]{:S(2)}) collective-permute-start(bf16[896,256]{1,0:T(8,128)(2,1)S(1)} %collective-permute-done.2.refs_1_), channel_id=1, source_target_pairs={{32,0},{48,16},{64,32},{80,48},{96,64},{112,80},{128,96},{144,112}... | collective-permute-start | bytes 1376264 | tf_op jit(solution)/shard_map/ppermute | solution.py:23
  80.4 19.0 %collective-permute-start.14 = (bf16[896,256]{1,0:T(8,128)(2,1)S(1)}, bf16[896,256]{1,0:T(8,128)(2,1)}, u32[]{:S(2)}, u32[]{:S(2)}) collective-permute-start(bf16[896,256]{1,0:T(8,128)(2,1)S(1)} %collective-permute-done.13.refs_15_), channel_id=1, source_target_pairs={{224,0},{240,16},{0,32},{16,48},{32,64},{48,80},{64,96},{80,112},{... | collective-permute-start | bytes 1376264 | tf_op jit(solution)/shard_map/ppermute | solution.py:23
  84.9 20.0 %collective-permute-start.7 = (bf16[896,256]{1,0:T(8,128)(2,1)S(1)}, bf16[896,256]{1,0:T(8,128)(2,1)}, u32[]{:S(2)}, u32[]{:S(2)}) collective-permute-start(bf16[896,256]{1,0:T(8,128)(2,1)S(1)} %collective-permute-done.6.refs_6_), channel_id=1, source_target_pairs={{224,0},{240,16},{0,32},{16,48},{32,64},{48,80},{64,96},{80,112},{... | collective-permute-start | bytes 1376264 | tf_op jit(solution)/shard_map/ppermute | solution.py:23
  85.8 19.7 %collective-permute-start.11 = (bf16[896,256]{1,0:T(8,128)(2,1)S(1)}, bf16[896,256]{1,0:T(8,128)(2,1)}, u32[]{:S(2)}, u32[]{:S(2)}) collective-permute-start(bf16[896,256]{1,0:T(8,128)(2,1)S(1)} %collective-permute-done.10.refs_10_), channel_id=1, source_target_pairs={{32,0},{48,16},{64,32},{80,48},{96,64},{112,80},{128,96},{144,112}... | collective-permute-start | bytes 1376264 | tf_op jit(solution)/shard_map/ppermute | solution.py:23
  95.6 19.8 %collective-permute-start.4 = (bf16[896,256]{1,0:T(8,128)(2,1)}, bf16[896,256]{1,0:T(8,128)(2,1)}, u32[]{:S(2)}, u32[]{:S(2)}) collective-permute-start(bf16[896,256]{1,0:T(8,128)(2,1)} %collective-permute-done.3.refs_2_), channel_id=1, source_target_pairs={{32,0},{48,16},{64,32},{80,48},{96,64},{112,80},{128,96},{144,112}... | collective-permute-start | bytes 1376264 | tf_op jit(solution)/shard_map/ppermute | solution.py:23
  99.4 16.0 %collective-permute-start.15 = (bf16[896,256]{1,0:T(8,128)(2,1)}, bf16[896,256]{1,0:T(8,128)(2,1)}, u32[]{:S(2)}, u32[]{:S(2)}) collective-permute-start(bf16[896,256]{1,0:T(8,128)(2,1)} %collective-permute-done.14.refs_14_), channel_id=1, source_target_pairs={{224,0},{240,16},{0,32},{16,48},{32,64},{48,80},{64,96},{80,112},{... | collective-permute-start | bytes 1376264 | tf_op jit(solution)/shard_map/ppermute | solution.py:23
  104.9 19.2 %collective-permute-start.8 = (bf16[896,256]{1,0:T(8,128)(2,1)}, bf16[896,256]{1,0:T(8,128)(2,1)}, u32[]{:S(2)}, u32[]{:S(2)}) collective-permute-start(bf16[896,256]{1,0:T(8,128)(2,1)} %collective-permute-done.7.refs_5_), channel_id=1, source_target_pairs={{224,0},{240,16},{0,32},{16,48},{32,64},{48,80},{64,96},{80,112},{... | collective-permute-start | bytes 1376264 | tf_op jit(solution)/shard_map/ppermute | solution.py:23
  105.4 19.3 %collective-permute-start.12 = (bf16[896,256]{1,0:T(8,128)(2,1)}, bf16[896,256]{1,0:T(8,128)(2,1)}, u32[]{:S(2)}, u32[]{:S(2)}) collective-permute-start(bf16[896,256]{1,0:T(8,128)(2,1)} %collective-permute-done.11.refs_11_), channel_id=1, source_target_pairs={{32,0},{48,16},{64,32},{80,48},{96,64},{112,80},{128,96},{144,112}... | collective-permute-start | bytes 1376264 | tf_op jit(solution)/shard_map/ppermute | solution.py:23
  128.9 44.5 %collective-permute-start.16 = (f32[2,896,256]{2,1,0:T(8,128)S(1)}, f32[2,896,256]{2,1,0:T(8,128)S(1)}, u32[]{:S(2)}, u32[]{:S(2)}) collective-permute-start(f32[2,896,256]{2,1,0:T(8,128)S(1)} %shard_map.78), channel_id=1, source_target_pairs={{0,16},{16,0},{32,48},{48,32},{64,80},{80,64},{96,112},{112,96},{1... | collective-permute-start | bytes 5505032 | tf_op jit(solution)/shard_map/ppermute | solution.py:27
  129.0 14.9 %collective-permute-start.17 = (bf16[896,256]{1,0:T(8,128)(2,1)S(1)}, bf16[896,256]{1,0:T(8,128)(2,1)S(1)}, u32[]{:S(2)}, u32[]{:S(2)}) collective-permute-start(bf16[896,256]{1,0:T(8,128)(2,1)S(1)} %copy-done.2), channel_id=1, source_target_pairs={{224,0},{240,16},{0,32},{16,48},{32,64},{48,80},{64,96},{80,112},{... | collective-permute-start | bytes 1376264 | tf_op jit(solution)/shard_map/ppermute | solution.py:23
  130.6 13.2 %collective-permute-start.21 = (bf16[896,256]{1,0:T(8,128)(2,1)S(1)}, bf16[896,256]{1,0:T(8,128)(2,1)S(1)}, u32[]{:S(2)}, u32[]{:S(2)}) collective-permute-start(bf16[896,256]{1,0:T(8,128)(2,1)S(1)} %copy-done.2), channel_id=1, source_target_pairs={{32,0},{48,16},{64,32},{80,48},{96,64},{112,80},{128,96},{144,112}... | collective-permute-start | bytes 1376264 | tf_op jit(solution)/shard_map/ppermute | solution.py:23
  143.9 13.5 %collective-permute-start.18 = (bf16[896,256]{1,0:T(8,128)(2,1)S(1)}, bf16[896,256]{1,0:T(8,128)(2,1)S(1)}, u32[]{:S(2)}, u32[]{:S(2)}) collective-permute-start(bf16[896,256]{1,0:T(8,128)(2,1)S(1)} %collective-permute-done.17.refs_1_), channel_id=1, source_target_pairs={{224,0},{240,16},{0,32},{16,48},{32,64},{48,80},{64,96},{80,112},{... | collective-permute-start | bytes 1376264 | tf_op jit(solution)/shard_map/ppermute | solution.py:23
  143.9 13.5 %collective-permute-start.22 = (bf16[896,256]{1,0:T(8,128)(2,1)S(1)}, bf16[896,256]{1,0:T(8,128)(2,1)S(1)}, u32[]{:S(2)}, u32[]{:S(2)}) collective-permute-start(bf16[896,256]{1,0:T(8,128)(2,1)S(1)} %collective-permute-done.21.refs_2_), channel_id=1, source_target_pairs={{32,0},{48,16},{64,32},{80,48},{96,64},{112,80},{128,96},{144,112}... | collective-permute-start | bytes 1376264 | tf_op jit(solution)/shard_map/ppermute | solution.py:23
  157.3 12.6 %collective-permute-start.19 = (bf16[896,256]{1,0:T(8,128)(2,1)S(1)}, bf16[896,256]{1,0:T(8,128)(2,1)S(1)}, u32[]{:S(2)}, u32[]{:S(2)}) collective-permute-start(bf16[896,256]{1,0:T(8,128)(2,1)S(1)} %collective-permute-done.18.refs_3_), channel_id=1, source_target_pairs={{224,0},{240,16},{0,32},{16,48},{32,64},{48,80},{64,96},{80,112},{... | collective-permute-start | bytes 1376264 | tf_op jit(solution)/shard_map/ppermute | solution.py:23
  157.3 12.7 %collective-permute-start.23 = (bf16[896,256]{1,0:T(8,128)(2,1)S(1)}, bf16[896,256]{1,0:T(8,128)(2,1)S(1)}, u32[]{:S(2)}, u32[]{:S(2)}) collective-permute-start(bf16[896,256]{1,0:T(8,128)(2,1)S(1)} %collective-permute-done.22.refs_4_), channel_id=1, source_target_pairs={{32,0},{48,16},{64,32},{80,48},{96,64},{112,80},{128,96},{144,112}... | collective-permute-start | bytes 1376264 | tf_op jit(solution)/shard_map/ppermute | solution.py:23
  187.3 24.4 %all-to-all-start.1 = ((bf16[16,128,256]{2,1,0:T(8,128)(2,1)}), bf16[16,128,256]{2,1,0:T(8,128)(2,1)}, u32[]{:S(2)}, u32[]{:S(2)}) async-start(bf16[16,128,256]{2,1,0:T(8,128)(2,1)} %shard_map.80), calls=%async_computation.1 | async-start | bytes 2097152 | tf_op jit(solution)/shard_map/all_to_all | solution.py:220
  211.7 23.4 %all-to-all-start.2 = ((bf16[16,128,256]{2,1,0:T(8,128)(2,1)}), bf16[16,128,256]{2,1,0:T(8,128)(2,1)S(1)}, u32[]{:S(2)}, u32[]{:S(2)}) async-start(bf16[16,128,256]{2,1,0:T(8,128)(2,1)} %shard_map.84), calls=%async_computation.2 | async-start | bytes 2097152 | tf_op jit(solution)/shard_map/all_to_all | solution.py:220
  (26 other events, 183.3 us)

commit v2 on v1

--- a/solution.py
+++ b/solution.py
@@ -13,6 +13,8 @@
 RING = 8
 FAR = 4
 TILE = 256
+CUT = 512
+SPLIT = (5, 3)
 NEAR = (0, 7, 1, 6, 2, 5, 3)
 F32 = jnp.float32
 BF16 = jnp.bfloat16
@@ -40,17 +42,20 @@
     return math.prod(shape) * jnp.dtype(dtype).itemsize
 
 
-def call(body, outs, scalars, *arrays):
+def call(body, outs, scalars, *arrays, loaded=(), scratch=(), aliases=None):
     specs = [pl.BlockSpec(memory_space=pltpu.SMEM)]
     specs += [pl.BlockSpec(memory_space=pltpu.VMEM)] * len(arrays)
-    held = sum(size(a.shape, a.dtype) for a in arrays) + sum(size(*o) for o in outs)
+    specs += [pl.BlockSpec(memory_space=pl.ANY)] * len(loaded)
+    held = sum(size(a.shape, a.dtype) for a in arrays + tuple(loaded)) + sum(size(*o) for o in outs)
     return pl.pallas_call(
         body,
         out_shape=[jax.ShapeDtypeStruct(s, d) for s, d in outs],
         in_specs=specs,
-        out_specs=[pl.BlockSpec(memory_space=pltpu.VMEM)] * len(outs),
-        compiler_params=pltpu.CompilerParams(vmem_limit_bytes=held + (4 << 20)),
-    )(scalars, *arrays)
+        out_specs=[pl.BlockSpec(memory_space=pl.ANY if aliases else pltpu.VMEM)] * len(outs),
+        scratch_shapes=list(scratch),
+        input_output_aliases=aliases or {},
+        compiler_params=pltpu.CompilerParams(vmem_limit_bytes=held + (6 << 20)),
+    )(scalars, *arrays, *loaded)
 
 
 CORE, SLOT, CHIP = 0, 1, 1 + RING
@@ -81,16 +86,33 @@
             out[which, lo:hi] = sum(dot(weights[k][lo:hi], x[k]) for k in range(RING))
 
 
+def pieces_of(refs, split):
+    refs, found = list(refs), {}
+    for k in NEAR:
+        if k in split:
+            low, high = refs.pop(0), refs.pop(0)
+            found[k] = [(0, CUT, low), (CUT, CUT + high.shape[0], high)]
+        else:
+            ref = refs.pop(0)
+            found[k] = [(0, ref.shape[0], ref)]
+    return found
+
+
+def rows_of(parts, lo, hi):
+    for at, end, ref in parts:
+        if at <= lo and hi <= end:
+            return ref[lo - at : hi - at]
+
+
 def grad_hidden_kernel(table, dy, *refs):
-    downs, out = refs[:-1], refs[-1]
+    downs, out = pieces_of(refs[:-1], SPLIT), refs[-1]
     for lo, hi in tiles(out.shape[0], TILE):
-        out[lo:hi] = sum(dot(downs[n][lo:hi], dy[k]) for n, k in enumerate(NEAR))
+        out[lo:hi] = sum(dot(rows_of(downs[k], lo, hi), dy[k]) for k in NEAR)
 
 
 def grad_hidden_far(table, dy, near, far_a, far_b, out):
-    cut = far_a.shape[0]
-    out[:cut] = near[:cut] + dot(far_a[...], dy[FAR])
-    out[cut:] = near[cut:] + dot(far_b[...], dy[FAR])
+    out[:CUT] = near[:CUT] + dot(far_a[...], dy[FAR])
+    out[CUT:] = near[CUT:] + dot(far_b[...], dy[FAR])
 
 
 def keep_and_give(table, k, block, keep, give):
@@ -107,25 +129,40 @@
         give[k] = block[:rows]
 
 
-def outputs_kernel(table, hidden_t, far_a, far_b, *refs):
-    downs, (keep, give, hidden) = refs[:-3], refs[-3:]
-    cut = far_a.shape[0]
+def outputs_near(table, hidden_t, *refs):
+    downs, (keep, give, hidden) = pieces_of(refs[:-3], SPLIT), refs[-3:]
     hidden[...] = hidden_t[...].T
-    for n, k in enumerate(NEAR):
-        keep_and_give(table, k, dot(hidden[...], downs[n][...]).astype(BF16), keep, give)
-    far = dot(hidden[:, :cut], far_a[...]) + dot(hidden[:, cut:], far_b[...])
-    keep_and_give(table, FAR, far.astype(BF16), keep, give)
+    for k in NEAR:
+        block = sum(dot(hidden[:, lo:hi], ref[...]) for lo, hi, ref in downs[k])
+        keep_and_give(table, k, block.astype(BF16), keep, give)
+
+
+def outputs_far(table, hidden, far_a, far_b, keep_in, give_in, keep, give, block, sems):
+    far = dot(hidden[:, :CUT], far_a[...]) + dot(hidden[:, CUT:], far_b[...])
+    far = far.astype(BF16)
+    keep_and_give(table, 0, far, block.at[0:1], block.at[1:2])
+    copies = [pltpu.make_async_copy(block.at[i], out.at[FAR], sems.at[i]) for i, out in enumerate((keep, give))]
+    for copy in copies:
+        copy.start()
+    for copy in copies:
+        copy.wait()
 
 
 def input_grads_kernel(table, mine, other, by_gate, by_up, *refs):
-    gates, ups = refs[:RING], refs[RING : 2 * RING]
-    keep, give, gg, gu = refs[2 * RING :]
+    weights, (keep, give, gg, gu, held, sems) = refs[: 2 * RING], refs[2 * RING :]
+    copies = []
+    for n in range(RING):
+        for i in (n, RING + n):
+            copies.append(pltpu.make_async_copy(weights[i], held.at[i], sems.at[i]))
+            copies[-1].start()
     for lo, hi in tiles(mine.shape[0], TILE):
         grad_hidden = mine[lo:hi] + other[lo:hi]
         gg[:, lo:hi] = (grad_hidden * by_gate[lo:hi]).astype(BF16).T
         gu[:, lo:hi] = (grad_hidden * by_up[lo:hi]).astype(BF16).T
     for k in range(RING):
-        block = dot(gg[...], gates[k][...]) + dot(gu[...], ups[k][...])
+        copies[2 * k].wait()
+        copies[2 * k + 1].wait()
+        block = dot(gg[...], held[k]) + dot(gu[...], held[RING + k])
         keep_and_give(table, k, block.astype(BF16), keep, give)
 
 
@@ -146,31 +183,31 @@
     rank = lax.axis_index("dp")
     z, c = rank // 2, rank % 2
 
-    def around(own, after=None):
+    def around(own, hops):
         right, left = [own], [own]
-        for n in range(3):
-            next_r, next_l = right[-1], left[-1]
-            if n == 1 and after:
-                next_r, _ = lax.optimization_barrier((next_r, after[0]))
-                next_l, _ = lax.optimization_barrier((next_l, after[1]))
-            right.append(ring(next_r, 1))
-            left.append(ring(next_l, -1))
+        for _ in range(hops):
+            right.append(ring(right[-1], 1))
+            left.append(ring(left[-1], -1))
         return right, left
 
-    g_r, g_l = around(gate_weight.T)
-    u_r, u_l = around(up_weight.T)
-    g_far, u_far = ring(g_r[3], 1), ring(u_l[3], -1)
-    d_r, d_l = around(down_weight, (g_r[3], g_l[3]))
-    cut = 512
-    d_far = (ring(d_r[3][:cut], 1), ring(d_l[3][cut:], -1))
+    g_r, g_l = around(gate_weight.T, 3)
+    u_r, u_l = around(up_weight.T, 3)
+    d_r, d_l = around(down_weight, 2)
+    g_far = ring(g_r[3], 1)
+    u_far = ring(u_l[3], -1)
+    d_r3a = ring(d_r[2][:CUT], 1)
+    d_l3b = ring(d_l[2][CUT:], -1)
+    d_r3b = ring(d_r[2][CUT:], 1)
+    d_l3a = ring(d_l[2][:CUT], -1)
+    d_far = (ring(d_r3a, 1), ring(d_l3b, -1))
 
     def by_delta(r, l, far):
         return [r[0], l[1], l[2], l[3], far, r[3], r[2], r[1]]
 
     gates = by_delta(g_r, g_l, g_far)
     ups = by_delta(u_r, u_l, u_far)
-    downs = by_delta(d_r, d_l, None)
-    near_downs = [downs[k] for k in NEAR]
+    downs = {0: [down_weight], 7: [d_r[1]], 1: [d_l[1]], 6: [d_r[2]], 2: [d_l[2]], 5: [d_r3a, d_r3b], 3: [d_l3a, d_l3b]}
+    near_downs = [piece for k in NEAR for piece in downs[k]]
 
     rank_count = lax.axis_size("dp")
     blocks = tokens.shape[0] // BLOCK
@@ -205,7 +242,8 @@
     by_row = (ff, 2 * rows)
     turned = ((2 * rows, ff), BF16)
     parts = call(gate_up_kernel, [((2,) + by_row, F32)], table, x_all, *gates, *ups)[0]
-    sums = parts + swap(parts)
+    parts_other = swap(parts)
+    sums = parts + parts_other
     gate_pre, up_pre = sums[0], sums[1]
     sigmoid_gate = jax.nn.sigmoid(gate_pre)
     activated = gate_pre * sigmoid_gate
@@ -216,17 +254,27 @@
 
     def reduce_columns(keep, give):
         share_of = ((2 * RING, rows, columns), BF16)
-        blocks_for = call(arrange_columns, [share_of], table, keep, swap(give))[0]
+        got_cols = swap(give)
+        blocks_for = call(arrange_columns, [share_of], table, keep, got_cols)[0]
         got_blocks = lax.all_to_all(blocks_for, "tensor", 0, 0, tiled=True)
         return jnp.sum(got_blocks.astype(F32), axis=0)
 
     grad_near = call(grad_hidden_kernel, [(by_row, F32)], table, dy_all, *near_downs)[0]
+    out_near = call(outputs_near, [half, half, turned], table, hidden, *near_downs)
     grad_part = call(grad_hidden_far, [(by_row, F32)], table, dy_all, grad_near, *d_far)[0]
     grad_other = swap(grad_part)
-    out = call(outputs_kernel, [half, half, turned], table, hidden, *d_far, *near_downs)
-    out_sum = reduce_columns(out[0], out[1])
-    dx = call(input_grads_kernel, [half, half, turned, turned], table, grad_part, grad_other, by_gate, activated, *gates, *ups)
-    dx_sum = reduce_columns(dx[0], dx[1])
+    out = call(
+        outputs_far, [half, half], table, out_near[2], *d_far, loaded=out_near[:2],
+        scratch=[pltpu.VMEM((2, rows, columns), BF16), pltpu.SemaphoreType.DMA((2,))], aliases={4: 0, 5: 1},
+    )
+    out_sum = reduce_columns(*out)
+    scratch = [pltpu.VMEM(*turned), pltpu.VMEM(*turned)]
+    scratch += [pltpu.VMEM((2 * RING, ff, columns), BF16), pltpu.SemaphoreType.DMA((2 * RING,))]
+    dx = call(
+        input_grads_kernel, [half, half], table, grad_part, grad_other, by_gate, activated,
+        loaded=gates + ups, scratch=scratch,
+    )
+    dx_sum = reduce_columns(*dx)
 
     back_pos = own_blocks + slot_ids
     back_ok = back_pos < share

time: 249 us -> 248 us (level)
    ppermute x22 -> x24, waiting for transfers between devices: 75.5 us -> 72 us  [ring(): return lax.ppermute(block, 'dp', route)]
    ppermute x2, starting transfers between devices: 10.9 us -> 7.73 us  [opposite(): return lax.ppermute(block, 'dp', [((d + n // 2) % n, d) for d in range(n)])]
    ppermute x22 -> x24, starting transfers between devices: 38.9 us -> 41.2 us  [ring(): return lax.ppermute(block, 'dp', route)]
    pallas_call x8 -> x9, Pallas kernels: 25.9 us -> 26.4 us  [call(): pl.pallas_call(body, out_shape=[jax.ShapeDtypeStruct(s, d) for s, d in ou...]
    unnamed x40 -> x38, local copies, waits for them, and re-layouts: 11.6 us -> 11.7 us
  transfers between devices with their start and end apart: 31 -> 33, of which waited for: 19 -> 17; matrix products, arithmetic and copies ran while one was open for 4% -> 4% of each run, Pallas kernels for 7% -> 9%
where the time goes in v2:
time: 248 us; the launch traced here: 246 us
  waiting for transfers between devices  96.8 us (39%)
  starting transfers between devices  62.6 us (25%)
  blocking collectives  34.1 us (14%)
  Pallas kernels  26.4 us (11%)
  local copies, waits for them, and re-layouts  16.1 us (6%)
  other arithmetic  7.02 us (3%)
  between operations  3.01 us (1%)
    ppermute x24, waiting for transfers between devices, ring(): return lax.ppermute(block, 'dp', route)  72 us
    ppermute x24, starting transfers between devices, ring(): return lax.ppermute(block, 'dp', route)  41.2 us
    all_to_all x1, blocking collectives, per_device(): every = lax.all_to_all(spread, 'tensor', 0, 0, tiled=True)  34.1 us
    pallas_call x9, Pallas kernels, call(): pl.pallas_call(body, out_shape=[jax.ShapeDtypeStruct(s, d) for s, d in ou...  26.4 us
    all_to_all x2, waiting for transfers between devices, reduce_columns(): got_blocks = lax.all_to_all(blocks_for, 'tensor', 0, 0, tiled=True)  14 us
    all_to_all x2, starting transfers between devices, reduce_columns(): got_blocks = lax.all_to_all(blocks_for, 'tensor', 0, 0, tiled=True)  12.8 us
    unnamed x38, local copies, waits for them, and re-layouts  11.7 us
    ppermute x2, waiting for transfers between devices, opposite(): return lax.ppermute(block, 'dp', [((d + n // 2) % n, d) for d in range(n)])  8.88 us
  transfers between devices with their start and end apart: 33, of which 17 were waited for; matrix products, arithmetic and copies ran while one was open for 4% of the time, Pallas kernels for 9%

profile of v2, /device:TPU:2, one launch (start us, length us, event | category | flops | bytes accessed | tf_op | source)
XLA Modules:
  0.0 246.1 jit_solution(16914068320491726762)
XLA Ops:
  1.6 7.3 %collective-permute-start = (bf16[2,128,256]{2,1,0:T(8,128)(2,1)S(1)}, bf16[2,128,256]{2,1,0:T(8,128)(2,1)S(1)}, u32[]{:S(2)}, u32[]{:S(2)}) collective-permute-start(bf16[2,128,256]{2,1,0:T(8,128)(2,1)S(1)} %pad_maximum_fusion.2), channel_id=1, source_target_pairs={{128,0},{144,16},{160,32},{176,48},{192,64},{208,80},{224,96},{240... | collective-permute-start | bytes 393224 | tf_op jit(solution)/shard_map/ppermute | solution.py:34
  15.2 34.1 %all_to_all.15.mine = bf16[16,2,256,128]{3,2,1,0:T(8,128)(2,1)S(1)} all-to-all(bf16[16,2,256,128]{3,2,1,0:T(8,128)(2,1)S(1)} %broadcast_in_dim.81), channel_id=1, replica_groups=mesh['dp'=16,'tensor'=16] {'tensor'}, dimensions={0} | all-to-all | bytes 4194304 | tf_op jit(solution)/shard_map/all_to_all | solution.py:234
  49.5 4.3 %collective-permute-start.9 = (bf16[896,256]{1,0:T(8,128)(2,1)S(1)}, bf16[896,256]{1,0:T(8,128)(2,1)S(1)}, u32[]{:S(2)}, u32[]{:S(2)}) collective-permute-start(bf16[896,256]{1,0:T(8,128)(2,1)S(1)} %bitcast.43), channel_id=1, source_target_pairs={{32,0},{48,16},{64,32},{80,48},{96,64},{112,80},{128,96},{144,112}... | collective-permute-start | bytes 1376264 | tf_op jit(solution)/shard_map/ppermute | solution.py:25
  58.5 6.3 %collective-permute-done.9.refs_9_ = bf16[896,256]{1,0:T(8,128)(2,1)S(1)} collective-permute-done((bf16[896,256]{1,0:T(8,128)(2,1)S(1)}, bf16[896,256]{1,0:T(8,128)(2,1)S(1)}, u32[]{:S(2)}, u32[]{:S(2)}) %collective-permute-start.9) | collective-permute-done | bytes 458784 | tf_op jit(solution)/shard_map/ppermute | solution.py:25
  64.8 3.7 %collective-permute-start.10 = (bf16[896,256]{1,0:T(8,128)(2,1)S(1)}, bf16[896,256]{1,0:T(8,128)(2,1)S(1)}, u32[]{:S(2)}, u32[]{:S(2)}) collective-permute-start(bf16[896,256]{1,0:T(8,128)(2,1)S(1)} %collective-permute-done.9.refs_9_), channel_id=1, source_target_pairs={{32,0},{48,16},{64,32},{80,48},{96,64},{112,80},{128,96},{144,112}... | collective-permute-start | bytes 1376264 | tf_op jit(solution)/shard_map/ppermute | solution.py:25
  70.6 9.0 %collective-permute-done.13.refs_15_ = bf16[896,256]{1,0:T(8,128)(2,1)S(1)} collective-permute-done((bf16[896,256]{1,0:T(8,128)(2,1)S(1)}, bf16[896,256]{1,0:T(8,128)(2,1)S(1)}, u32[]{:S(2)}, u32[]{:S(2)}) %collective-permute-start.13) | collective-permute-done | bytes 458784 | tf_op jit(solution)/shard_map/ppermute | solution.py:25
  84.4 3.7 %collective-permute-start.11 = (bf16[896,256]{1,0:T(8,128)(2,1)S(1)}, bf16[896,256]{1,0:T(8,128)(2,1)}, u32[]{:S(2)}, u32[]{:S(2)}) collective-permute-start(bf16[896,256]{1,0:T(8,128)(2,1)S(1)} %collective-permute-done.10.refs_10_), channel_id=1, source_target_pairs={{32,0},{48,16},{64,32},{80,48},{96,64},{112,80},{128,96},{144,112}... | collective-permute-start | bytes 1376264 | tf_op jit(solution)/shard_map/ppermute | solution.py:25
  90.2 9.1 %collective-permute-done.14.refs_14_ = bf16[896,256]{1,0:T(8,128)(2,1)} collective-permute-done((bf16[896,256]{1,0:T(8,128)(2,1)S(1)}, bf16[896,256]{1,0:T(8,128)(2,1)}, u32[]{:S(2)}, u32[]{:S(2)}) %collective-permute-start.14) | collective-permute-done | bytes 458784 | tf_op jit(solution)/shard_map/ppermute | solution.py:25
  104.4 3.8 %collective-permute-start.12 = (bf16[896,256]{1,0:T(8,128)(2,1)}, bf16[896,256]{1,0:T(8,128)(2,1)}, u32[]{:S(2)}, u32[]{:S(2)}) collective-permute-start(bf16[896,256]{1,0:T(8,128)(2,1)} %collective-permute-done.11.refs_11_), channel_id=1, source_target_pairs={{32,0},{48,16},{64,32},{80,48},{96,64},{112,80},{128,96},{144,112}... | collective-permute-start | bytes 1376264 | tf_op jit(solution)/shard_map/ppermute | solution.py:25
  111.5 7.6 %collective-permute-done.15.refs_13_ = bf16[896,256]{1,0:T(8,128)(2,1)} collective-permute-done((bf16[896,256]{1,0:T(8,128)(2,1)}, bf16[896,256]{1,0:T(8,128)(2,1)}, u32[]{:S(2)}, u32[]{:S(2)}) %collective-permute-start.15) | collective-permute-done | bytes 458784 | tf_op jit(solution)/shard_map/ppermute | solution.py:25
  119.0 4.4 %collective-permute-done.12.refs_12_ = bf16[896,256]{1,0:T(8,128)(2,1)} collective-permute-done((bf16[896,256]{1,0:T(8,128)(2,1)}, bf16[896,256]{1,0:T(8,128)(2,1)}, u32[]{:S(2)}, u32[]{:S(2)}) %collective-permute-start.12) | collective-permute-done | bytes 458784 | tf_op jit(solution)/shard_map/ppermute | solution.py:25
  123.4 4.7 %collective-permute-done.8.refs_4_ = bf16[896,256]{1,0:T(8,128)(2,1)} collective-permute-done((bf16[896,256]{1,0:T(8,128)(2,1)}, bf16[896,256]{1,0:T(8,128)(2,1)}, u32[]{:S(2)}, u32[]{:S(2)}) %collective-permute-start.8) | collective-permute-done | bytes 458784 | tf_op jit(solution)/shard_map/ppermute | solution.py:25
  128.2 4.1 %shard_map.78 = f32[2,896,256]{2,1,0:T(8,128)S(1)} custom-call(s32[10]{0:T(128)S(1)} %pad_add_fusion.table, bf16[8,256,256]{2,1,0:T(8,128)(2,1)S(1)} %get-tuple-element.11.x, bf16[896,256]{1,0:T(8,128)(2,1)S(1)} %bitcast.49, bf16[896,256]{1,0:T(8,128)(2,1)S(1)} %copy-done.9, bf16[896,256]{1,0:T(8,128)(2,1)} %collective-permute-done.3.refs_2_, ...), custom_call_target="tpu_custom_call" | custom-call | tf_op jit(solution)/shard_map/pallas_call | solution.py:50
  135.7 10.8 %collective-permute-done.17.refs_1_ = bf16[896,256]{1,0:T(8,128)(2,1)S(1)} collective-permute-done((bf16[896,256]{1,0:T(8,128)(2,1)S(1)}, bf16[896,256]{1,0:T(8,128)(2,1)S(1)}, u32[]{:S(2)}, u32[]{:S(2)}) %collective-permute-start.17) | collective-permute-done | bytes 458784 | tf_op jit(solution)/shard_map/ppermute | solution.py:25
  146.5 3.2 %collective-permute-start.20 = (bf16[896,256]{1,0:T(8,128)(2,1)S(1)}, bf16[896,256]{1,0:T(8,128)(2,1)S(1)}, u32[]{:S(2)}, u32[]{:S(2)}) collective-permute-start(bf16[896,256]{1,0:T(8,128)(2,1)S(1)} %collective-permute-done.18.refs_2_), channel_id=1, source_target_pairs={{32,0},{48,16},{64,32},{80,48},{96,64},{112,80},{128,96},{144,112}... | collective-permute-start | bytes 1376264 | tf_op jit(solution)/shard_map/ppermute | solution.py:25
  149.8 9.9 %collective-permute-done.19.refs_3_ = bf16[896,256]{1,0:T(8,128)(2,1)S(1)} collective-permute-done((bf16[896,256]{1,0:T(8,128)(2,1)S(1)}, bf16[896,256]{1,0:T(8,128)(2,1)S(1)}, u32[]{:S(2)}, u32[]{:S(2)}) %collective-permute-start.19) | collective-permute-done | bytes 458784 | tf_op jit(solution)/shard_map/ppermute | solution.py:25
  159.9 3.3 %collective-permute-start.24 = (bf16[384,256]{1,0:T(8,128)(2,1)S(1)}, bf16[384,256]{1,0:T(8,128)(2,1)S(1)}, u32[]{:S(2)}, u32[]{:S(2)}) collective-permute-start(bf16[384,256]{1,0:T(8,128)(2,1)S(1)} %slice.59), channel_id=1, source_target_pairs={{32,0},{48,16},{64,32},{80,48},{96,64},{112,80},{128,96},{144,112}... | collective-permute-start | bytes 589832 | tf_op jit(solution)/shard_map/ppermute | solution.py:25
  168.4 3.7 %collective-permute-start.26 = (bf16[384,256]{1,0:T(8,128)(2,1)S(1)}, bf16[384,256]{1,0:T(8,128)(2,1)S(1)}, u32[]{:S(2)}, u32[]{:S(2)}) collective-permute-start(bf16[384,256]{1,0:T(8,128)(2,1)S(1)} %collective-permute-done.24.refs_8_), channel_id=1, source_target_pairs={{32,0},{48,16},{64,32},{80,48},{96,64},{112,80},{128,96},{144,112}... | collective-permute-start | bytes 589832 | tf_op jit(solution)/shard_map/ppermute | solution.py:25
  173.8 3.5 %shard_map.79 = (bf16[8,128,256]{2,1,0:T(8,128)(2,1)S(1)}, bf16[8,128,256]{2,1,0:T(8,128)(2,1)S(1)}, bf16[256,896]{1,0:T(8,128)(2,1)S(1)}) custom-call(s32[10]{0:T(128)S(1)} %pad_add_fusion.table, bf16[896,256]{1,0:T(8,128)(2,1)S(1)} %get-tuple-element.24.hidden_t, bf16[896,256]{1,0:T(8,128)(2,1)S(1)} %copy-done.1, ...), custom_call_target="tpu_custom_call" | custom-call | tf_op jit(solution)/shard_map/pallas_call | solution.py:50
  185.7 5.5 %all-to-all-start.1 = ((bf16[16,128,256]{2,1,0:T(8,128)(2,1)}), bf16[16,128,256]{2,1,0:T(8,128)(2,1)}, u32[]{:S(2)}, u32[]{:S(2)}) async-start(bf16[16,128,256]{2,1,0:T(8,128)(2,1)} %shard_map.81), calls=%async_computation.1 | async-start | bytes 2097152 | tf_op jit(solution)/shard_map/all_to_all | solution.py:259
  197.5 9.6 %shard_map.84 = (bf16[8,128,256]{2,1,0:T(8,128)(2,1)S(1)}, bf16[8,128,256]{2,1,0:T(8,128)(2,1)S(1)}) custom-call(s32[10]{0:T(128)S(1)} %pad_add_fusion.table, f32[896,256]{1,0:T(8,128)S(1)} %shard_map.83.mine, f32[896,256]{1,0:T(8,128)} %collective-permute-done.28.other, f32[896,256]{1,0:T(8,128)S(1)} %copy-done, f32[896,256]{1,0:T(8,128)S(1)} %get-tuple-element.25.by_up, ...), custom_call_target="tpu_custom_call" | custom-call | tf_op jit(solution)/shard_map/pallas_call | solution.py:50
  211.0 7.3 %all-to-all-start.2 = ((bf16[16,128,256]{2,1,0:T(8,128)(2,1)}), bf16[16,128,256]{2,1,0:T(8,128)(2,1)S(1)}, u32[]{:S(2)}, u32[]{:S(2)}) async-start(bf16[16,128,256]{2,1,0:T(8,128)(2,1)} %shard_map.85), calls=%async_computation.2 | async-start | bytes 2097152 | tf_op jit(solution)/shard_map/all_to_all | solution.py:259
  220.3 14.0 %all-to-all-done.2 = bf16[16,128,256]{2,1,0:T(8,128)(2,1)S(1)} async-done(((bf16[16,128,256]{2,1,0:T(8,128)(2,1)}), bf16[16,128,256]{2,1,0:T(8,128)(2,1)S(1)}, u32[]{:S(2)}, u32[]{:S(2)}) %all-to-all-start.2) | async-done | bytes 1048608 | tf_op jit(solution)/shard_map/all_to_all | solution.py:259
  236.4 8.9 %collective-permute-done.30 = bf16[2,8,16,256]{3,2,0,1:T(8,128)(2,1)S(1)} collective-permute-done((bf16[2,8,16,256]{3,2,0,1:T(8,128)(2,1)S(1)}, bf16[2,8,16,256]{3,2,0,1:T(8,128)(2,1)S(1)}, u32[]{:S(2)}, u32[]{:S(2)}) %collective-permute-start.30) | collective-permute-done | bytes 131104 | tf_op jit(solution)/shard_map/ppermute | solution.py:34
  (126 shorter events, 61.1 us)
Async XLA Ops:
  1.6 12.2 %collective-permute-start = (bf16[2,128,256]{2,1,0:T(8,128)(2,1)S(1)}, bf16[2,128,256]{2,1,0:T(8,128)(2,1)S(1)}, u32[]{:S(2)}, u32[]{:S(2)}) collective-permute-start(bf16[2,128,256]{2,1,0:T(8,128)(2,1)S(1)} %pad_maximum_fusion.2), channel_id=1, source_target_pairs={{128,0},{144,16},{160,32},{176,48},{192,64},{208,80},{224,96},{240... | collective-permute-start | bytes 393224 | tf_op jit(solution)/shard_map/ppermute | solution.py:34
  49.3 60.0 %collective-permute-start.1 = (bf16[16,2,256,128]{3,2,1,0:T(8,128)(2,1)S(1)}, bf16[16,2,256,128]{3,2,1,0:T(8,128)(2,1)}, u32[]{:S(2)}, u32[]{:S(2)}) collective-permute-start(bf16[16,2,256,128]{3,2,1,0:T(8,128)(2,1)S(1)} %all_to_all.15.mine), channel_id=1, source_target_pairs={{0,16},{16,0},{32,48},{48,32},{64,80},{80,64},{96,112},{112,96},{1... | collective-permute-start | bytes 6291464 | tf_op jit(solution)/shard_map/ppermute | solution.py:29
  49.5 15.2 %collective-permute-start.9 = (bf16[896,256]{1,0:T(8,128)(2,1)S(1)}, bf16[896,256]{1,0:T(8,128)(2,1)S(1)}, u32[]{:S(2)}, u32[]{:S(2)}) collective-permute-start(bf16[896,256]{1,0:T(8,128)(2,1)S(1)} %bitcast.43), channel_id=1, source_target_pairs={{32,0},{48,16},{64,32},{80,48},{96,64},{112,80},{128,96},{144,112}... | collective-permute-start | bytes 1376264 | tf_op jit(solution)/shard_map/ppermute | solution.py:25
  55.1 14.7 %collective-permute-start.5 = (bf16[896,256]{1,0:T(8,128)(2,1)S(1)}, bf16[896,256]{1,0:T(8,128)(2,1)S(1)}, u32[]{:S(2)}, u32[]{:S(2)}) collective-permute-start(bf16[896,256]{1,0:T(8,128)(2,1)S(1)} %bitcast.47), channel_id=1, source_target_pairs={{224,0},{240,16},{0,32},{16,48},{32,64},{48,80},{64,96},{80,112},{... | collective-permute-start | bytes 1376264 | tf_op jit(solution)/shard_map/ppermute | solution.py:25
  55.2 24.4 %collective-permute-start.13 = (bf16[896,256]{1,0:T(8,128)(2,1)S(1)}, bf16[896,256]{1,0:T(8,128)(2,1)S(1)}, u32[]{:S(2)}, u32[]{:S(2)}) collective-permute-start(bf16[896,256]{1,0:T(8,128)(2,1)S(1)} %bitcast.44), channel_id=1, source_target_pairs={{224,0},{240,16},{0,32},{16,48},{32,64},{48,80},{64,96},{80,112},{... | collective-permute-start | bytes 1376264 | tf_op jit(solution)/shard_map/ppermute | solution.py:25
  55.3 25.2 %collective-permute-start.2 = (bf16[896,256]{1,0:T(8,128)(2,1)S(1)}, bf16[896,256]{1,0:T(8,128)(2,1)S(1)}, u32[]{:S(2)}, u32[]{:S(2)}) collective-permute-start(bf16[896,256]{1,0:T(8,128)(2,1)S(1)} %bitcast.48), channel_id=1, source_target_pairs={{32,0},{48,16},{64,32},{80,48},{96,64},{112,80},{128,96},{144,112}... | collective-permute-start | bytes 1376264 | tf_op jit(solution)/shard_map/ppermute | solution.py:25
  64.8 19.7 %collective-permute-start.10 = (bf16[896,256]{1,0:T(8,128)(2,1)S(1)}, bf16[896,256]{1,0:T(8,128)(2,1)S(1)}, u32[]{:S(2)}, u32[]{:S(2)}) collective-permute-start(bf16[896,256]{1,0:T(8,128)(2,1)S(1)} %collective-permute-done.9.refs_9_), channel_id=1, source_target_pairs={{32,0},{48,16},{64,32},{80,48},{96,64},{112,80},{128,96},{144,112}... | collective-permute-start | bytes 1376264 | tf_op jit(solution)/shard_map/ppermute | solution.py:25
  69.8 19.7 %collective-permute-start.6 = (bf16[896,256]{1,0:T(8,128)(2,1)S(1)}, bf16[896,256]{1,0:T(8,128)(2,1)S(1)}, u32[]{:S(2)}, u32[]{:S(2)}) collective-permute-start(bf16[896,256]{1,0:T(8,128)(2,1)S(1)} %collective-permute-done.5.refs_7_), channel_id=1, source_target_pairs={{224,0},{240,16},{0,32},{16,48},{32,64},{48,80},{64,96},{80,112},{... | collective-permute-start | bytes 1376264 | tf_op jit(solution)/shard_map/ppermute | solution.py:25
  79.6 19.8 %collective-permute-start.14 = (bf16[896,256]{1,0:T(8,128)(2,1)S(1)}, bf16[896,256]{1,0:T(8,128)(2,1)}, u32[]{:S(2)}, u32[]{:S(2)}) collective-permute-start(bf16[896,256]{1,0:T(8,128)(2,1)S(1)} %collective-permute-done.13.refs_15_), channel_id=1, source_target_pairs={{224,0},{240,16},{0,32},{16,48},{32,64},{48,80},{64,96},{80,112},{... | collective-permute-start | bytes 1376264 | tf_op jit(solution)/shard_map/ppermute | solution.py:25
  80.4 18.9 %collective-permute-start.3 = (bf16[896,256]{1,0:T(8,128)(2,1)S(1)}, bf16[896,256]{1,0:T(8,128)(2,1)}, u32[]{:S(2)}, u32[]{:S(2)}) collective-permute-start(bf16[896,256]{1,0:T(8,128)(2,1)S(1)} %collective-permute-done.2.refs_1_), channel_id=1, source_target_pairs={{32,0},{48,16},{64,32},{80,48},{96,64},{112,80},{128,96},{144,112}... | collective-permute-start | bytes 1376264 | tf_op jit(solution)/shard_map/ppermute | solution.py:25
  84.4 20.0 %collective-permute-start.11 = (bf16[896,256]{1,0:T(8,128)(2,1)S(1)}, bf16[896,256]{1,0:T(8,128)(2,1)}, u32[]{:S(2)}, u32[]{:S(2)}) collective-permute-start(bf16[896,256]{1,0:T(8,128)(2,1)S(1)} %collective-permute-done.10.refs_10_), channel_id=1, source_target_pairs={{32,0},{48,16},{64,32},{80,48},{96,64},{112,80},{128,96},{144,112}... | collective-permute-start | bytes 1376264 | tf_op jit(solution)/shard_map/ppermute | solution.py:25
  89.4 19.8 %collective-permute-start.7 = (bf16[896,256]{1,0:T(8,128)(2,1)S(1)}, bf16[896,256]{1,0:T(8,128)(2,1)}, u32[]{:S(2)}, u32[]{:S(2)}) collective-permute-start(bf16[896,256]{1,0:T(8,128)(2,1)S(1)} %collective-permute-done.6.refs_6_), channel_id=1, source_target_pairs={{224,0},{240,16},{0,32},{16,48},{32,64},{48,80},{64,96},{80,112},{... | collective-permute-start | bytes 1376264 | tf_op jit(solution)/shard_map/ppermute | solution.py:25
  99.4 19.7 %collective-permute-start.15 = (bf16[896,256]{1,0:T(8,128)(2,1)}, bf16[896,256]{1,0:T(8,128)(2,1)}, u32[]{:S(2)}, u32[]{:S(2)}) collective-permute-start(bf16[896,256]{1,0:T(8,128)(2,1)} %collective-permute-done.14.refs_14_), channel_id=1, source_target_pairs={{224,0},{240,16},{0,32},{16,48},{32,64},{48,80},{64,96},{80,112},{... | collective-permute-start | bytes 1376264 | tf_op jit(solution)/shard_map/ppermute | solution.py:25
  99.4 19.7 %collective-permute-start.4 = (bf16[896,256]{1,0:T(8,128)(2,1)}, bf16[896,256]{1,0:T(8,128)(2,1)}, u32[]{:S(2)}, u32[]{:S(2)}) collective-permute-start(bf16[896,256]{1,0:T(8,128)(2,1)} %collective-permute-done.3.refs_2_), channel_id=1, source_target_pairs={{32,0},{48,16},{64,32},{80,48},{96,64},{112,80},{128,96},{144,112}... | collective-permute-start | bytes 1376264 | tf_op jit(solution)/shard_map/ppermute | solution.py:25
  104.4 19.0 %collective-permute-start.12 = (bf16[896,256]{1,0:T(8,128)(2,1)}, bf16[896,256]{1,0:T(8,128)(2,1)}, u32[]{:S(2)}, u32[]{:S(2)}) collective-permute-start(bf16[896,256]{1,0:T(8,128)(2,1)} %collective-permute-done.11.refs_11_), channel_id=1, source_target_pairs={{32,0},{48,16},{64,32},{80,48},{96,64},{112,80},{128,96},{144,112}... | collective-permute-start | bytes 1376264 | tf_op jit(solution)/shard_map/ppermute | solution.py:25
  109.2 18.9 %collective-permute-start.8 = (bf16[896,256]{1,0:T(8,128)(2,1)}, bf16[896,256]{1,0:T(8,128)(2,1)}, u32[]{:S(2)}, u32[]{:S(2)}) collective-permute-start(bf16[896,256]{1,0:T(8,128)(2,1)} %collective-permute-done.7.refs_5_), channel_id=1, source_target_pairs={{224,0},{240,16},{0,32},{16,48},{32,64},{48,80},{64,96},{80,112},{... | collective-permute-start | bytes 1376264 | tf_op jit(solution)/shard_map/ppermute | solution.py:25
  132.3 39.9 %collective-permute-start.16 = (f32[2,896,256]{2,1,0:T(8,128)S(1)}, f32[2,896,256]{2,1,0:T(8,128)S(1)}, u32[]{:S(2)}, u32[]{:S(2)}) collective-permute-start(f32[2,896,256]{2,1,0:T(8,128)S(1)} %shard_map.78), channel_id=1, source_target_pairs={{0,16},{16,0},{32,48},{48,32},{64,80},{80,64},{96,112},{112,96},{1... | collective-permute-start | bytes 5505032 | tf_op jit(solution)/shard_map/ppermute | solution.py:29
  132.4 14.1 %collective-permute-start.17 = (bf16[896,256]{1,0:T(8,128)(2,1)S(1)}, bf16[896,256]{1,0:T(8,128)(2,1)S(1)}, u32[]{:S(2)}, u32[]{:S(2)}) collective-permute-start(bf16[896,256]{1,0:T(8,128)(2,1)S(1)} %copy-done.1), channel_id=1, source_target_pairs={{224,0},{240,16},{0,32},{16,48},{32,64},{48,80},{64,96},{80,112},{... | collective-permute-start | bytes 1376264 | tf_op jit(solution)/shard_map/ppermute | solution.py:25
  132.5 14.0 %collective-permute-start.18 = (bf16[896,256]{1,0:T(8,128)(2,1)S(1)}, bf16[896,256]{1,0:T(8,128)(2,1)S(1)}, u32[]{:S(2)}, u32[]{:S(2)}) collective-permute-start(bf16[896,256]{1,0:T(8,128)(2,1)S(1)} %copy-done.1), channel_id=1, source_target_pairs={{32,0},{48,16},{64,32},{80,48},{96,64},{112,80},{128,96},{144,112}... | collective-permute-start | bytes 1376264 | tf_op jit(solution)/shard_map/ppermute | solution.py:25
  146.5 13.2 %collective-permute-start.19 = (bf16[896,256]{1,0:T(8,128)(2,1)S(1)}, bf16[896,256]{1,0:T(8,128)(2,1)S(1)}, u32[]{:S(2)}, u32[]{:S(2)}) collective-permute-start(bf16[896,256]{1,0:T(8,128)(2,1)S(1)} %collective-permute-done.17.refs_1_), channel_id=1, source_target_pairs={{224,0},{240,16},{0,32},{16,48},{32,64},{48,80},{64,96},{80,112},{... | collective-permute-start | bytes 1376264 | tf_op jit(solution)/shard_map/ppermute | solution.py:25
  146.5 13.3 %collective-permute-start.20 = (bf16[896,256]{1,0:T(8,128)(2,1)S(1)}, bf16[896,256]{1,0:T(8,128)(2,1)S(1)}, u32[]{:S(2)}, u32[]{:S(2)}) collective-permute-start(bf16[896,256]{1,0:T(8,128)(2,1)S(1)} %collective-permute-done.18.refs_2_), channel_id=1, source_target_pairs={{32,0},{48,16},{64,32},{80,48},{96,64},{112,80},{128,96},{144,112}... | collective-permute-start | bytes 1376264 | tf_op jit(solution)/shard_map/ppermute | solution.py:25
  159.7 12.4 %collective-permute-start.21 = (bf16[512,256]{1,0:T(8,128)(2,1)S(1)}, bf16[512,256]{1,0:T(8,128)(2,1)S(1)}, u32[]{:S(2)}, u32[]{:S(2)}) collective-permute-start(bf16[512,256]{1,0:T(8,128)(2,1)S(1)} %slice.56), channel_id=1, source_target_pairs={{224,0},{240,16},{0,32},{16,48},{32,64},{48,80},{64,96},{80,112},{... | collective-permute-start | bytes 786440 | tf_op jit(solution)/shard_map/ppermute | solution.py:25
  185.7 25.3 %all-to-all-start.1 = ((bf16[16,128,256]{2,1,0:T(8,128)(2,1)}), bf16[16,128,256]{2,1,0:T(8,128)(2,1)}, u32[]{:S(2)}, u32[]{:S(2)}) async-start(bf16[16,128,256]{2,1,0:T(8,128)(2,1)} %shard_map.81), calls=%async_computation.1 | async-start | bytes 2097152 | tf_op jit(solution)/shard_map/all_to_all | solution.py:259
  211.0 23.4 %all-to-all-start.2 = ((bf16[16,128,256]{2,1,0:T(8,128)(2,1)}), bf16[16,128,256]{2,1,0:T(8,128)(2,1)S(1)}, u32[]{:S(2)}, u32[]{:S(2)}) async-start(bf16[16,128,256]{2,1,0:T(8,128)(2,1)} %shard_map.85), calls=%async_computation.2 | async-start | bytes 2097152 | tf_op jit(solution)/shard_map/all_to_all | solution.py:259
  (27 other events, 212.0 us)

commit v3 on v2

v3 whole, which is shorter than its diff:
```python
import functools
import math

import jax
import jax.numpy as jnp
from jax import lax
from jax.experimental import pallas as pl
from jax.experimental.pallas import tpu as pltpu
from jax.sharding import PartitionSpec as P


BLOCK = 16
SIDE = 4
RING = 8
TILE = 256
ARRIVAL = (0, 7, 1, 6, 2, 5, 3, 4)
NEAR = RING - 1
EARLY = 5
F32 = jnp.float32
BF16 = jnp.bfloat16


def ring(block, step):
    route = [(((d // 2 - step) % RING) * 2 + d % 2, d) for d in range(2 * RING)]
    return lax.ppermute(block, "dp", route)


def swap(block):
    return lax.ppermute(block, "dp", [(d, d ^ 1) for d in range(2 * RING)])


def opposite(block):
    n = 2 * RING
    return lax.ppermute(block, "dp", [((d + n // 2) % n, d) for d in range(n)])


def dot(left, right):
    return jnp.dot(left, right, preferred_element_type=F32)


def dot_t(left, right):
    return lax.dot_general(left, right, (((1,), (1,)), ((), ())), preferred_element_type=F32)


def size(shape, dtype):
    return math.prod(shape) * jnp.dtype(dtype).itemsize


def call(body, outs, scalars, *arrays, loaded=(), scratch=(), aliases=None):
    specs = [pl.BlockSpec(memory_space=pltpu.SMEM)]
    specs += [pl.BlockSpec(memory_space=pltpu.VMEM)] * len(arrays)
    specs += [pl.BlockSpec(memory_space=pl.ANY)] * len(loaded)
    held = sum(size(a.shape, a.dtype) for a in arrays) + sum(size(*o) for o in outs)
    return pl.pallas_call(
        body,
        out_shape=[jax.ShapeDtypeStruct(s, d) for s, d in outs],
        in_specs=specs,
        out_specs=[pl.BlockSpec(memory_space=pl.ANY if aliases else pltpu.VMEM)] * len(outs),
        scratch_shapes=list(scratch),
        input_output_aliases=aliases or {},
        compiler_params=pltpu.CompilerParams(vmem_limit_bytes=held + (6 << 20) + (8 << 20 if len(loaded) > RING else 0)),
    )(scalars, *arrays, *loaded)


CORE, SLOT, PLACE = 0, 1, 1 + RING


def loop(count, body):
    lax.fori_loop(0, count, lambda i, carry: (body(i), carry)[1], 0)


def tile_loop(extent, body):
    full = extent // TILE
    loop(full, lambda i: body(pl.ds(pl.multiple_of(i * TILE, TILE), TILE)))
    if extent % TILE:
        body(slice(full * TILE, extent))


def arrange_features(table, mine, other, x_out, dy_out):
    rows = mine.shape[2]
    at = pl.multiple_of(table[CORE] * rows, rows)
    away = pl.multiple_of((1 - table[CORE]) * rows, rows)

    def one(n):
        slot = table[SLOT + n]
        for which, out in ((0, x_out), (1, dy_out)):
            out[n, pl.ds(at, rows), :] = mine[slot, which]
            out[n, pl.ds(away, rows), :] = other[slot, which]

    loop(RING, one)


def fetch(refs, held, sems):
    copies = [pltpu.make_async_copy(ref, held.at[i], sems.at[i]) for i, ref in enumerate(refs)]
    for copy in copies:
        copy.start()


def fetched(held, sems, i):
    pltpu.make_async_copy(held.at[i], held.at[i], sems.at[i]).wait()


def early_sums(table, x, *refs, turned):
    weights, (out, held, sems) = refs[:-3], refs[-3:]
    fetch(weights, held, sems)
    loop(EARLY, lambda i: fetched(held, sems, i))

    def tile(part):
        if turned:
            out[:, part] = sum(dot_t(x[n], held[n, part, :]) for n in range(EARLY))
        else:
            out[:, part] = sum(dot(x[n], held[n, :, part]) for n in range(EARLY))

    tile_loop(out.shape[1], tile)


def gate_up_late(table, x, gate_early, up_early, *refs):
    weights, (out, give, held, sems) = refs[:-4], refs[-4:]
    late = RING - EARLY
    fetch(weights, held, sems)
    loop(2 * late, lambda i: fetched(held, sems, i))

    def tile(part):
        for which, early in enumerate((gate_early, up_early)):
            more = sum(dot_t(x[EARLY + n], held[which * late + n, part, :]) for n in range(late))
            total = early[:, part] + more
            out[which, :, part] = total
            give[which, :, part] = total.astype(BF16)

    tile_loop(out.shape[2], tile)


def grad_late(table, dy, early, *refs):
    downs, (out, held, sems) = refs[:-3], refs[-3:]
    late = NEAR - EARLY
    fetch(downs, held, sems)
    loop(late, lambda i: fetched(held, sems, i))

    def tile(part):
        out[:, part] = early[:, part] + sum(dot(dy[EARLY + n], held[n, :, part]) for n in range(late))

    tile_loop(out.shape[1], tile)


def grad_hidden_far(table, dy, near, far, out):
    def tile(part):
        out[:, part] = near[:, part] + dot(dy[NEAR], far[:, part])

    tile_loop(out.shape[1], tile)


def keep_and_give(table, n, block, both, keep, give):
    rows = keep.shape[1]
    both[...] = block.astype(BF16)
    keep[n] = both[pl.ds(pl.multiple_of(table[CORE] * rows, rows), rows), :]
    give[n] = both[pl.ds(pl.multiple_of((1 - table[CORE]) * rows, rows), rows), :]


def outputs_kernel(table, mine, other, early, late, far, keep, give, hidden, both):
    def tile(part):
        gate_pre = mine[0, :, part] + other[0, :, part].astype(F32)
        up_pre = mine[1, :, part] + other[1, :, part].astype(F32)
        activated = gate_pre * jax.nn.sigmoid(gate_pre)
        hidden[:, part] = (activated * up_pre).astype(BF16)

    tile_loop(hidden.shape[1], tile)
    loop(EARLY, lambda n: keep_and_give(table, n, dot_t(hidden[...], early[n]), both, keep, give))
    more = NEAR - EARLY
    loop(more, lambda n: keep_and_give(table, EARLY + n, dot_t(hidden[...], late[n]), both, keep, give))
    keep_and_give(table, NEAR, dot_t(hidden[...], far[...]), both, keep, give)


def input_grads_kernel(table, mine, other, by_gate, by_up, *refs):
    weights, (keep, give, gg, gu, both, held, sems) = refs[: 2 * RING], refs[2 * RING :]
    fetch(weights, held, sems)

    def tile(part):
        grad_hidden = mine[:, part] + other[:, part]
        gg[:, part] = (grad_hidden * by_gate[:, part]).astype(BF16)
        gu[:, part] = (grad_hidden * by_up[:, part]).astype(BF16)

    tile_loop(mine.shape[1], tile)

    def one(n):
        fetched(held, sems, 2 * n)
        fetched(held, sems, 2 * n + 1)
        keep_and_give(table, n, dot(gg[...], held[2 * n]) + dot(gu[...], held[2 * n + 1]), both, keep, give)

    loop(RING, one)


def arrange_columns(table, mine, other, out):
    def one(chip):
        place = table[PLACE + chip]
        out[2 * chip + table[CORE]] = mine[place]
        out[2 * chip + 1 - table[CORE]] = other[place]

    loop(RING, one)


def finish_kernel(table, got, done, back):
    share = done.shape[0]

    def add(j):
        part = pl.ds(pl.multiple_of(j * BLOCK, BLOCK), BLOCK)
        total = sum(got[s, part, :].astype(F32) for s in range(got.shape[0]))
        done[j] = jnp.where(table[j] != 0, total, 0.0).astype(BF16)

    def send(j):
        block = done[table[2 * share + j]].astype(F32)
        back[j] = jnp.where(table[share + j] != 0, block, 0.0).astype(BF16)

    loop(share, add)
    loop(share, send)


def per_device(tokens, cotangent, gate_weight, up_weight, down_weight, counts):
    rank = lax.axis_index("dp")
    z, c = rank // 2, rank % 2

    def around(own, hops):
        right, left = [own], [own]
        for _ in range(hops):
            right.append(ring(right[-1], 1))
            left.append(ring(left[-1], -1))
        return right, left

    g_r, g_l = around(gate_weight.T, 3)
    u_r, u_l = around(up_weight.T, 3)
    d_r, d_l = around(down_weight.T, 3)
    g_far = ring(g_r[3], 1)
    u_far = ring(u_l[3], -1)
    d_far = ring(d_l[3], -1)

    def near_of(r, l):
        slices = {0: r[0], 1: l[1], 2: l[2], 3: l[3], 5: r[3], 6: r[2], 7: r[1]}
        return [slices[k] for k in ARRIVAL[:-1]]

    rank_count = lax.axis_size("dp")
    blocks = tokens.shape[0] // BLOCK
    columns = tokens.shape[1]
    own_blocks = counts[rank]
    share = blocks // 2
    rows = share * BLOCK
    partner_count = counts[(rank + rank_count // 2) % rank_count]
    got = opposite(jnp.stack([tokens[rows:], cotangent[rows:]]))
    keep_blocks = jnp.minimum(own_blocks, share)
    slot_ids = jnp.arange(share, dtype=jnp.int32)
    foreign = slot_ids - own_blocks
    mine = slot_ids < keep_blocks
    valid = mine | (foreign >= 0) & (foreign < partner_count - share)
    source_index = jnp.where(mine, slot_ids, share + jnp.clip(foreign, 0, share - 1))
    lower = jnp.stack([tokens[:rows], cotangent[:rows]])
    stacked = jnp.concatenate([lower.reshape(2, share, BLOCK, columns), got.reshape(2, share, BLOCK, columns)], axis=1)
    pieces = jnp.take(stacked, source_index, axis=1)
    pieces = jnp.where(valid[None, :, None, None], pieces, jnp.zeros_like(pieces))
    work = pieces.reshape(2, rows, columns)

    spread = jnp.broadcast_to(work[None], (SIDE * SIDE, *work.shape))
    every = lax.all_to_all(spread, "tensor", 0, 0, tiled=True)
    slots = 2 * ((z + jnp.array(ARRIVAL, jnp.int32)) % RING) + c
    order = jnp.array([ARRIVAL.index(k) for k in range(RING)], jnp.int32)
    places = lax.dynamic_slice_in_dim(jnp.concatenate([order, order]), (RING - z) % RING, RING)
    every_other = swap(every)
    table = jnp.concatenate([c[None], slots, places]).astype(jnp.int32)
    wide = (RING, 2 * rows, columns)
    x_all, dy_all = call(arrange_features, [(wide, BF16)] * 2, table, every, every_other)

    ff = gate_weight.shape[1]
    by_row = (2 * rows, ff)

    def arrivals(count):
        return [pltpu.SemaphoreType.DMA((count,))]

    def early_of(x, slices, turned, keep=False):
        held = (EARLY, *slices[0].shape)
        return call(
            functools.partial(early_sums, turned=turned),
            [(by_row, F32)] + [(held, BF16)] * keep, table, x, loaded=slices[:EARLY],
            scratch=[pltpu.VMEM(held, BF16)] * (not keep) + arrivals(EARLY),
        )

    gate_all, up_all = near_of(g_r, g_l) + [g_far], near_of(u_r, u_l) + [u_far]
    gate_early = early_of(x_all, gate_all, True)[0]
    up_early = early_of(x_all, up_all, True)[0]
    late = RING - EARLY
    parts, parts_give = call(
        gate_up_late, [((2,) + by_row, F32), ((2,) + by_row, BF16)], table, x_all, gate_early, up_early,
        loaded=gate_all[EARLY:] + up_all[EARLY:],
        scratch=[pltpu.VMEM((2 * late, ff, columns), BF16)] + arrivals(2 * late),
    )
    parts_other = swap(parts_give)
    sums = parts + parts_other.astype(F32)
    gate_pre, up_pre = sums[0], sums[1]
    sigmoid_gate = jax.nn.sigmoid(gate_pre)
    activated = gate_pre * sigmoid_gate
    by_gate = up_pre * sigmoid_gate * (1.0 + gate_pre * (1.0 - sigmoid_gate))

    eight = ((RING, rows, columns), BF16)
    both = pltpu.VMEM((2 * rows, columns), BF16)

    def reduce_columns(keep, give):
        share_of = ((2 * RING, rows, columns), BF16)
        got_cols = swap(give)
        blocks_for = call(arrange_columns, [share_of], table, keep, got_cols)[0]
        return lax.all_to_all(blocks_for, "tensor", 0, 0, tiled=True)

    down_near = near_of(d_r, d_l)
    grad_early, down_early = early_of(dy_all, down_near, False, keep=True)
    grad_near, down_late = call(
        grad_late, [(by_row, F32), ((NEAR - EARLY, columns, ff), BF16)], table, dy_all, grad_early,
        loaded=down_near[EARLY:], scratch=arrivals(NEAR - EARLY),
    )
    grad_part = call(grad_hidden_far, [(by_row, F32)], table, dy_all, grad_near, d_far)[0]
    grad_other = swap(grad_part)
    out = call(
        outputs_kernel, [eight, eight], table, parts, parts_other, down_early, down_late, d_far,
        scratch=[pltpu.VMEM(by_row, BF16), both],
    )
    out_sum = reduce_columns(*out)
    pairs = zip(near_of(g_r, g_l) + [g_far], near_of(u_r, u_l) + [u_far])
    dx_weights = [w for pair in pairs for w in pair]
    scratch = [pltpu.VMEM(by_row, BF16)] * 2 + [both, pltpu.VMEM((2 * RING, ff, columns), BF16)] + arrivals(2 * RING)
    dx = call(
        input_grads_kernel, [eight, eight], table, grad_part, grad_other, by_gate, activated,
        loaded=dx_weights, scratch=scratch,
    )
    dx_sum = reduce_columns(*dx)

    back_pos = own_blocks + slot_ids
    back_ok = back_pos < share
    back_index = jnp.clip(back_pos, 0, share - 1)
    upper_live = slot_ids < own_blocks - share

    blocks_table = jnp.concatenate([valid, back_ok, back_index]).astype(jnp.int32)

    def home(got_blocks):
        eight_blocks = ((share, BLOCK, columns), BF16)
        done, back = call(finish_kernel, [eight_blocks] * 2, blocks_table, got_blocks)
        returned = opposite(back)
        low = jnp.where(mine[:, None, None], done, jnp.zeros_like(done))
        high = jnp.where(upper_live[:, None, None], returned, jnp.zeros_like(returned))
        return jnp.concatenate([low, high], axis=0).reshape(2 * rows, columns)

    return home(out_sum), home(dx_sum)


def solution(mesh):
    in_specs = (
        P("dp", "tensor"),
        P("dp", "tensor"),
        P("dp", "tensor"),
        P("dp", "tensor"),
        P("tensor", "dp"),
        P(),
    )
    out_specs = (P("dp", "tensor"), P("dp", "tensor"))

    return jax.shard_map(per_device, mesh=mesh, in_specs=in_specs, out_specs=out_specs, check_vma=False)
```

time: 248 us -> 228 us (0.919)
  waiting for transfers between devices: 96.8 us -> 74.1 us
  Pallas kernels: 26.4 us -> 36.7 us
  local copies, waits for them, and re-layouts: 16.1 us -> 9.51 us
    ppermute x24 -> x21, waiting for transfers between devices: 72 us -> 55.3 us  [ring(): return lax.ppermute(block, 'dp', route)]
    pallas_call x9 -> x13, Pallas kernels: 26.4 us -> 36.7 us  [call(): pl.pallas_call(body, out_shape=[jax.ShapeDtypeStruct(s, d) for s, d in ou...]
    ppermute x2 -> x3, starting transfers between devices: 7.73 us -> 14.7 us  [opposite(): return lax.ppermute(block, 'dp', [((d + n // 2) % n, d) for d in range(n)])]
    unnamed x38 -> x37, local copies, waits for them, and re-layouts: 11.7 us -> 6.05 us
    ppermute x2 -> x3, waiting for transfers between devices: 8.88 us -> 4.74 us  [opposite(): return lax.ppermute(block, 'dp', [((d + n // 2) % n, d) for d in range(n)])]
    ppermute x24 -> x21, starting transfers between devices: 41.2 us -> 37.7 us  [ring(): return lax.ppermute(block, 'dp', route)]
    all_to_all x2, starting transfers between devices: 12.8 us -> 10.1 us  [reduce_columns(): return lax.all_to_all(blocks_for, 'tensor', 0, 0, tiled=True)]
  transfers between devices with their start and end apart: 33 -> 31, of which waited for: 17 -> 17; matrix products, arithmetic and copies ran while one was open for 4% -> 4% of each run, Pallas kernels for 9% -> 15%
where the time goes in v3:
time: 228 us; the launch traced here: 227 us
  waiting for transfers between devices  74.1 us (32%)
  starting transfers between devices  63.3 us (28%)
  Pallas kernels  36.7 us (16%)
  blocking collectives  34.1 us (15%)
  local copies, waits for them, and re-layouts  9.51 us (4%)
  other arithmetic  6.17 us (3%)
  between operations  3.02 us (1%)
    ppermute x21, waiting for transfers between devices, ring(): return lax.ppermute(block, 'dp', route)  55.3 us
    ppermute x21, starting transfers between devices, ring(): return lax.ppermute(block, 'dp', route)  37.7 us
    pallas_call x13, Pallas kernels, call(): pl.pallas_call(body, out_shape=[jax.ShapeDtypeStruct(s, d) for s, d in ou...  36.7 us
    all_to_all x1, blocking collectives, per_device(): every = lax.all_to_all(spread, 'tensor', 0, 0, tiled=True)  34.1 us
    ppermute x3, starting transfers between devices, opposite(): return lax.ppermute(block, 'dp', [((d + n // 2) % n, d) for d in range(n)])  14.7 us
    all_to_all x2, waiting for transfers between devices, reduce_columns(): return lax.all_to_all(blocks_for, 'tensor', 0, 0, tiled=True)  12.2 us
    all_to_all x2, starting transfers between devices, reduce_columns(): return lax.all_to_all(blocks_for, 'tensor', 0, 0, tiled=True)  10.1 us
    unnamed x37, local copies, waits for them, and re-layouts  6.05 us
  transfers between devices with their start and end apart: 31, of which 17 were waited for; matrix products, arithmetic and copies ran while one was open for 4% of the time, Pallas kernels for 15%

profile of v3, /device:TPU:2, one launch (start us, length us, event | category | flops | bytes accessed | tf_op | source)
XLA Modules:
  0.0 227.0 jit_solution(18059511505831239822)
XLA Ops:
  1.6 7.3 %collective-permute-start = (bf16[2,128,256]{2,1,0:T(8,128)(2,1)S(1)}, bf16[2,128,256]{2,1,0:T(8,128)(2,1)S(1)}, u32[]{:S(2)}, u32[]{:S(2)}) collective-permute-start(bf16[2,128,256]{2,1,0:T(8,128)(2,1)S(1)} %pad_maximum_fusion.1), channel_id=1, source_target_pairs={{128,0},{144,16},{160,32},{176,48},{192,64},{208,80},{224,96},{240... | collective-permute-start | bytes 393224 | tf_op jit(solution)/shard_map/ppermute | solution.py:34
  14.2 34.1 %all_to_all.15.mine = bf16[16,2,128,256]{3,2,1,0:T(8,128)(2,1)S(1)} all-to-all(bf16[16,2,128,256]{3,2,1,0:T(8,128)(2,1)S(1)} %broadcast_in_dim.71), channel_id=1, replica_groups=mesh['dp'=16,'tensor'=16] {'tensor'}, dimensions={0} | all-to-all | bytes 4194304 | tf_op jit(solution)/shard_map/all_to_all | solution.py:260
  49.8 3.8 %collective-permute-start.3 = (bf16[896,256]{1,0:T(8,128)(2,1)S(1)}, bf16[896,256]{1,0:T(8,128)(2,1)}, u32[]{:S(2)}, u32[]{:S(2)}) collective-permute-start(bf16[896,256]{1,0:T(8,128)(2,1)S(1)} %bitcast.35), channel_id=1, source_target_pairs={{32,0},{48,16},{64,32},{80,48},{96,64},{112,80},{128,96},{144,112}... | collective-permute-start | bytes 1376264 | tf_op jit(solution)/shard_map/ppermute | solution.py:25
  60.1 4.7 %collective-permute-done.2.refs_1_.refs_2_ = bf16[896,256]{1,0:T(8,128)(2,1)S(1)} collective-permute-done((bf16[896,256]{1,0:T(8,128)(2,1)S(1)}, bf16[896,256]{1,0:T(8,128)(2,1)S(1)}, u32[]{:S(2)}, u32[]{:S(2)}) %collective-permute-start.2) | collective-permute-done | bytes 458784 | tf_op jit(solution)/shard_map/ppermute | solution.py:25
  68.3 6.5 %collective-permute-done.6.refs_1_.refs_3_ = bf16[896,256]{1,0:T(8,128)(2,1)} collective-permute-done((bf16[896,256]{1,0:T(8,128)(2,1)S(1)}, bf16[896,256]{1,0:T(8,128)(2,1)}, u32[]{:S(2)}, u32[]{:S(2)}) %collective-permute-start.6) | collective-permute-done | bytes 458784 | tf_op jit(solution)/shard_map/ppermute | solution.py:25
  78.1 6.4 %collective-permute-done.17.refs_1_ = bf16[256,896]{1,0:T(8,128)(2,1)S(1)} collective-permute-done((bf16[256,896]{1,0:T(8,128)(2,1)}, bf16[256,896]{1,0:T(8,128)(2,1)S(1)}, u32[]{:S(2)}, u32[]{:S(2)}) %collective-permute-start.17) | collective-permute-done | bytes 458784 | tf_op jit(solution)/shard_map/ppermute | solution.py:25
  86.7 7.7 %collective-permute-done.4.refs_3_.refs_6_ = bf16[896,256]{1,0:T(8,128)(2,1)S(1)} collective-permute-done((bf16[896,256]{1,0:T(8,128)(2,1)S(1)}, bf16[896,256]{1,0:T(8,128)(2,1)S(1)}, u32[]{:S(2)}, u32[]{:S(2)}) %collective-permute-start.4) | collective-permute-done | bytes 458784 | tf_op jit(solution)/shard_map/ppermute | solution.py:25
  99.2 4.7 %collective-permute-done.5.refs_4_.refs_8_ = bf16[896,256]{1,0:T(8,128)(2,1)} collective-permute-done((bf16[896,256]{1,0:T(8,128)(2,1)}, bf16[896,256]{1,0:T(8,128)(2,1)}, u32[]{:S(2)}, u32[]{:S(2)}) %collective-permute-start.5) | collective-permute-done | bytes 458784 | tf_op jit(solution)/shard_map/ppermute | solution.py:25
  103.9 3.7 %collective-permute-start.20 = (bf16[256,896]{1,0:T(8,128)(2,1)}, bf16[256,896]{1,0:T(8,128)(2,1)}, u32[]{:S(2)}, u32[]{:S(2)}) collective-permute-start(bf16[256,896]{1,0:T(8,128)(2,1)} %collective-permute-done.18.refs_2_), channel_id=1, source_target_pairs={{32,0},{48,16},{64,32},{80,48},{96,64},{112,80},{128,96},{144,112}... | collective-permute-start | bytes 1376264 | tf_op jit(solution)/shard_map/ppermute | solution.py:25
  108.5 5.4 %collective-permute-done.10.refs_0_.refs_10_ = bf16[896,256]{1,0:T(8,128)(2,1)} collective-permute-done((bf16[896,256]{1,0:T(8,128)(2,1)S(1)}, bf16[896,256]{1,0:T(8,128)(2,1)}, u32[]{:S(2)}, u32[]{:S(2)}) %collective-permute-start.10) | collective-permute-done | bytes 458784 | tf_op jit(solution)/shard_map/ppermute | solution.py:25
  119.6 3.9 %shard_map.96.gate_early = f32[256,896]{1,0:T(8,128)S(1)} custom-call(s32[17]{0:T(128)S(1)} %pad_add_fusion.1.table, bf16[8,256,256]{2,1,0:T(8,128)(2,1)S(1)} %get-tuple-element.18.x, bf16[896,256]{1,0:T(8,128)(2,1)S(1)} %bitcast.36, bf16[896,256]{1,0:T(8,128)(2,1)S(1)} %collective-permute-done.2.refs_1_.refs_2_, ...), custom_call_target="tpu_custom_call" | custom-call | tf_op jit(solution)/shard_map/pallas_call | solution.py:54
  123.5 3.6 %shard_map.97.up_early = f32[256,896]{1,0:T(8,128)S(1)} custom-call(s32[17]{0:T(128)S(1)} %pad_add_fusion.1.table, bf16[8,256,256]{2,1,0:T(8,128)(2,1)S(1)} %get-tuple-element.18.x, bf16[896,256]{1,0:T(8,128)(2,1)S(1)} %bitcast.40, bf16[896,256]{1,0:T(8,128)(2,1)} %collective-permute-done.6.refs_1_.refs_3_, ...), custom_call_target="tpu_custom_call" | custom-call | tf_op jit(solution)/shard_map/pallas_call | solution.py:54
  127.2 6.2 %collective-permute-done.11.refs_1_.refs_12_ = bf16[896,256]{1,0:T(8,128)(2,1)} collective-permute-done((bf16[896,256]{1,0:T(8,128)(2,1)}, bf16[896,256]{1,0:T(8,128)(2,1)}, u32[]{:S(2)}, u32[]{:S(2)}) %collective-permute-start.11) | collective-permute-done | bytes 458784 | tf_op jit(solution)/shard_map/ppermute | solution.py:25
  133.4 3.7 %collective-permute-start.22 = (bf16[256,896]{1,0:T(8,128)(2,1)}, bf16[256,896]{1,0:T(8,128)(2,1)S(1)}, u32[]{:S(2)}, u32[]{:S(2)}) collective-permute-start(bf16[256,896]{1,0:T(8,128)(2,1)} %collective-permute-done.20.refs_4_), channel_id=1, source_target_pairs={{32,0},{48,16},{64,32},{80,48},{96,64},{112,80},{128,96},{144,112}... | collective-permute-start | bytes 1376264 | tf_op jit(solution)/shard_map/ppermute | solution.py:25
  138.7 4.6 %collective-permute-done.15.refs_5_.refs_15_ = bf16[896,256]{1,0:T(8,128)(2,1)} collective-permute-done((bf16[896,256]{1,0:T(8,128)(2,1)}, bf16[896,256]{1,0:T(8,128)(2,1)}, u32[]{:S(2)}, u32[]{:S(2)}) %collective-permute-start.15) | collective-permute-done | bytes 458784 | tf_op jit(solution)/shard_map/ppermute | solution.py:25
  143.3 3.9 %shard_map.98 = (f32[2,256,896]{2,1,0:T(8,128)S(1)}, bf16[2,256,896]{2,1,0:T(8,128)(2,1)S(1)}) custom-call(s32[17]{0:T(128)S(1)} %pad_add_fusion.1.table, bf16[8,256,256]{2,1,0:T(8,128)(2,1)S(1)} %get-tuple-element.18.x, f32[256,896]{1,0:T(8,128)S(1)} %shard_map.96.gate_early, f32[256,896]{1,0:T(8,128)S(1)} %shard_map.97.up_early, ...), custom_call_target="tpu_custom_call" | custom-call | tf_op jit(solution)/shard_map/pallas_call | solution.py:54
  156.2 3.8 %shard_map.99 = (f32[256,896]{1,0:T(8,128)S(1)}, bf16[5,256,896]{2,1,0:T(8,128)(2,1)S(1)}) custom-call(s32[17]{0:T(128)S(1)} %pad_add_fusion.1.table, bf16[8,256,256]{2,1,0:T(8,128)(2,1)S(1)} %get-tuple-element.21.x.dy, bf16[256,896]{1,0:T(8,128)(2,1)S(1)} %bitcast.44, bf16[256,896]{1,0:T(8,128)(2,1)S(1)} %copy-done.13, ...), custom_call_target="tpu_custom_call" | custom-call | tf_op jit(solution)/shard_map/pallas_call | solution.py:54
  173.9 4.9 %all-to-all-start.1 = ((bf16[16,128,256]{2,1,0:T(8,128)(2,1)}), bf16[16,128,256]{2,1,0:T(8,128)(2,1)S(1)}, u32[]{:S(2)}, u32[]{:S(2)}) async-start(bf16[16,128,256]{2,1,0:T(8,128)(2,1)} %shard_map.102), calls=%async_computation.1 | async-start | bytes 2097152 | tf_op jit(solution)/shard_map/all_to_all | solution.py:306
  181.6 6.8 %shard_map.105 = (bf16[8,128,256]{2,1,0:T(8,128)(2,1)S(1)}, bf16[8,128,256]{2,1,0:T(8,128)(2,1)S(1)}) custom-call(s32[17]{0:T(128)S(1)} %pad_add_fusion.1.table, f32[256,896]{1,0:T(8,128)} %shard_map.104.mine, f32[256,896]{1,0:T(8,128)} %collective-permute-done.26.other, f32[256,896]{1,0:T(8,128)S(1)} %get-tuple-element.37.by_gate, ...), custom_call_target="tpu_custom_call" | custom-call | tf_op jit(solution)/shard_map/pallas_call | solution.py:54
  195.2 5.2 %all-to-all-start.2 = ((bf16[16,128,256]{2,1,0:T(8,128)(2,1)}), bf16[16,128,256]{2,1,0:T(8,128)(2,1)S(1)}, u32[]{:S(2)}, u32[]{:S(2)}) async-start(bf16[16,128,256]{2,1,0:T(8,128)(2,1)} %shard_map.106), calls=%async_computation.2 | async-start | bytes 2097152 | tf_op jit(solution)/shard_map/all_to_all | solution.py:306
  203.3 3.7 %collective-permute-start.25 = (bf16[8,16,256]{2,1,0:T(8,128)(2,1)S(1)}, bf16[8,16,256]{2,1,0:T(8,128)(2,1)S(1)}, u32[]{:S(2)}, u32[]{:S(2)}) collective-permute-start(bf16[8,16,256]{2,1,0:T(8,128)(2,1)S(1)} %get-tuple-element.28), channel_id=1, source_target_pairs={{128,0},{144,16},{160,32},{176,48},{192,64},{208,80},{224,96},{240... | collective-permute-start | bytes 196616 | tf_op jit(solution)/shard_map/ppermute | solution.py:34
  207.0 9.2 %all-to-all-done.2.got = bf16[16,128,256]{2,1,0:T(8,128)(2,1)S(1)} async-done(((bf16[16,128,256]{2,1,0:T(8,128)(2,1)}), bf16[16,128,256]{2,1,0:T(8,128)(2,1)S(1)}, u32[]{:S(2)}, u32[]{:S(2)}) %all-to-all-start.2) | async-done | bytes 1048608 | tf_op jit(solution)/shard_map/all_to_all | solution.py:306
  217.0 3.7 %collective-permute-start.28 = (bf16[8,16,256]{2,1,0:T(8,128)(2,1)S(1)}, bf16[8,16,256]{2,1,0:T(8,128)(2,1)S(1)}, u32[]{:S(2)}, u32[]{:S(2)}) collective-permute-start(bf16[8,16,256]{2,1,0:T(8,128)(2,1)S(1)} %get-tuple-element.33), channel_id=1, source_target_pairs={{128,0},{144,16},{160,32},{176,48},{192,64},{208,80},{224,96},{240... | collective-permute-start | bytes 196616 | tf_op jit(solution)/shard_map/ppermute | solution.py:34
  220.8 4.7 %collective-permute-done.28 = bf16[8,16,256]{2,1,0:T(8,128)(2,1)S(1)} collective-permute-done((bf16[8,16,256]{2,1,0:T(8,128)(2,1)S(1)}, bf16[8,16,256]{2,1,0:T(8,128)(2,1)S(1)}, u32[]{:S(2)}, u32[]{:S(2)}) %collective-permute-start.28) | collective-permute-done | bytes 65568 | tf_op jit(solution)/shard_map/ppermute | solution.py:34
  (118 shorter events, 71.6 us)
Async XLA Ops:
  48.3 67.2 %collective-permute-start.1 = (bf16[16,2,128,256]{3,2,1,0:T(8,128)(2,1)S(1)}, bf16[16,2,128,256]{3,2,1,0:T(8,128)(2,1)}, u32[]{:S(2)}, u32[]{:S(2)}) collective-permute-start(bf16[16,2,128,256]{3,2,1,0:T(8,128)(2,1)S(1)} %all_to_all.15.mine), channel_id=1, source_target_pairs={{0,16},{16,0},{32,48},{48,32},{64,80},{80,64},{96,112},{112,96},{1... | collective-permute-start | bytes 6291464 | tf_op jit(solution)/shard_map/ppermute | solution.py:29
  48.5 16.3 %collective-permute-start.2 = (bf16[896,256]{1,0:T(8,128)(2,1)S(1)}, bf16[896,256]{1,0:T(8,128)(2,1)S(1)}, u32[]{:S(2)}, u32[]{:S(2)}) collective-permute-start(bf16[896,256]{1,0:T(8,128)(2,1)S(1)} %bitcast.34), channel_id=1, source_target_pairs={{224,0},{240,16},{0,32},{16,48},{32,64},{48,80},{64,96},{80,112},{... | collective-permute-start | bytes 1376264 | tf_op jit(solution)/shard_map/ppermute | solution.py:25
  49.8 15.1 %collective-permute-start.3 = (bf16[896,256]{1,0:T(8,128)(2,1)S(1)}, bf16[896,256]{1,0:T(8,128)(2,1)}, u32[]{:S(2)}, u32[]{:S(2)}) collective-permute-start(bf16[896,256]{1,0:T(8,128)(2,1)S(1)} %bitcast.35), channel_id=1, source_target_pairs={{32,0},{48,16},{64,32},{80,48},{96,64},{112,80},{128,96},{144,112}... | collective-permute-start | bytes 1376264 | tf_op jit(solution)/shard_map/ppermute | solution.py:25
  54.8 20.0 %collective-permute-start.6 = (bf16[896,256]{1,0:T(8,128)(2,1)S(1)}, bf16[896,256]{1,0:T(8,128)(2,1)}, u32[]{:S(2)}, u32[]{:S(2)}) collective-permute-start(bf16[896,256]{1,0:T(8,128)(2,1)S(1)} %bitcast.38), channel_id=1, source_target_pairs={{224,0},{240,16},{0,32},{16,48},{32,64},{48,80},{64,96},{80,112},{... | collective-permute-start | bytes 1376264 | tf_op jit(solution)/shard_map/ppermute | solution.py:25
  54.9 19.9 %collective-permute-start.7 = (bf16[896,256]{1,0:T(8,128)(2,1)S(1)}, bf16[896,256]{1,0:T(8,128)(2,1)}, u32[]{:S(2)}, u32[]{:S(2)}) collective-permute-start(bf16[896,256]{1,0:T(8,128)(2,1)S(1)} %bitcast.39), channel_id=1, source_target_pairs={{32,0},{48,16},{64,32},{80,48},{96,64},{112,80},{128,96},{144,112}... | collective-permute-start | bytes 1376264 | tf_op jit(solution)/shard_map/ppermute | solution.py:25
  64.9 19.7 %collective-permute-start.17 = (bf16[256,896]{1,0:T(8,128)(2,1)}, bf16[256,896]{1,0:T(8,128)(2,1)S(1)}, u32[]{:S(2)}, u32[]{:S(2)}) collective-permute-start(bf16[256,896]{1,0:T(8,128)(2,1)} %bitcast.42), channel_id=1, source_target_pairs={{224,0},{240,16},{0,32},{16,48},{32,64},{48,80},{64,96},{80,112},{... | collective-permute-start | bytes 1376264 | tf_op jit(solution)/shard_map/ppermute | solution.py:25
  64.9 21.8 %collective-permute-start.18 = (bf16[256,896]{1,0:T(8,128)(2,1)}, bf16[256,896]{1,0:T(8,128)(2,1)}, u32[]{:S(2)}, u32[]{:S(2)}) collective-permute-start(bf16[256,896]{1,0:T(8,128)(2,1)} %bitcast.43), channel_id=1, source_target_pairs={{32,0},{48,16},{64,32},{80,48},{96,64},{112,80},{128,96},{144,112}... | collective-permute-start | bytes 1376264 | tf_op jit(solution)/shard_map/ppermute | solution.py:25
  74.8 19.6 %collective-permute-start.4 = (bf16[896,256]{1,0:T(8,128)(2,1)S(1)}, bf16[896,256]{1,0:T(8,128)(2,1)S(1)}, u32[]{:S(2)}, u32[]{:S(2)}) collective-permute-start(bf16[896,256]{1,0:T(8,128)(2,1)S(1)} %collective-permute-done.2.refs_1_.refs_2_), channel_id=1, source_target_pairs={{224,0},{240,16},{0,32},{16,48},{32,64},{48,80},{64,96},{80,112},{... | collective-permute-start | bytes 1376264 | tf_op jit(solution)/shard_map/ppermute | solution.py:25
  74.8 20.4 %collective-permute-start.9 = (bf16[896,256]{1,0:T(8,128)(2,1)}, bf16[896,256]{1,0:T(8,128)(2,1)S(1)}, u32[]{:S(2)}, u32[]{:S(2)}) collective-permute-start(bf16[896,256]{1,0:T(8,128)(2,1)} %collective-permute-done.7.refs_2_.refs_5_), channel_id=1, source_target_pairs={{32,0},{48,16},{64,32},{80,48},{96,64},{112,80},{128,96},{144,112}... | collective-permute-start | bytes 1376264 | tf_op jit(solution)/shard_map/ppermute | solution.py:25
  84.5 19.4 %collective-permute-start.5 = (bf16[896,256]{1,0:T(8,128)(2,1)}, bf16[896,256]{1,0:T(8,128)(2,1)}, u32[]{:S(2)}, u32[]{:S(2)}) collective-permute-start(bf16[896,256]{1,0:T(8,128)(2,1)} %collective-permute-done.3.refs_2_.refs_4_), channel_id=1, source_target_pairs={{32,0},{48,16},{64,32},{80,48},{96,64},{112,80},{128,96},{144,112}... | collective-permute-start | bytes 1376264 | tf_op jit(solution)/shard_map/ppermute | solution.py:25
  86.7 21.0 %collective-permute-start.8 = (bf16[896,256]{1,0:T(8,128)(2,1)}, bf16[896,256]{1,0:T(8,128)(2,1)}, u32[]{:S(2)}, u32[]{:S(2)}) collective-permute-start(bf16[896,256]{1,0:T(8,128)(2,1)} %collective-permute-done.6.refs_1_.refs_3_), channel_id=1, source_target_pairs={{224,0},{240,16},{0,32},{16,48},{32,64},{48,80},{64,96},{80,112},{... | collective-permute-start | bytes 1376264 | tf_op jit(solution)/shard_map/ppermute | solution.py:25
  94.4 19.6 %collective-permute-start.10 = (bf16[896,256]{1,0:T(8,128)(2,1)S(1)}, bf16[896,256]{1,0:T(8,128)(2,1)}, u32[]{:S(2)}, u32[]{:S(2)}) collective-permute-start(bf16[896,256]{1,0:T(8,128)(2,1)S(1)} %collective-permute-done.4.refs_3_.refs_6_), channel_id=1, source_target_pairs={{224,0},{240,16},{0,32},{16,48},{32,64},{48,80},{64,96},{80,112},{... | collective-permute-start | bytes 1376264 | tf_op jit(solution)/shard_map/ppermute | solution.py:25
  95.2 18.8 %collective-permute-start.14 = (bf16[896,256]{1,0:T(8,128)(2,1)S(1)}, bf16[896,256]{1,0:T(8,128)(2,1)}, u32[]{:S(2)}, u32[]{:S(2)}) collective-permute-start(bf16[896,256]{1,0:T(8,128)(2,1)S(1)} %collective-permute-done.9.refs_4_.refs_9_), channel_id=1, source_target_pairs={{32,0},{48,16},{64,32},{80,48},{96,64},{112,80},{128,96},{144,112}... | collective-permute-start | bytes 1376264 | tf_op jit(solution)/shard_map/ppermute | solution.py:25
  103.9 23.2 %collective-permute-start.20 = (bf16[256,896]{1,0:T(8,128)(2,1)}, bf16[256,896]{1,0:T(8,128)(2,1)}, u32[]{:S(2)}, u32[]{:S(2)}) collective-permute-start(bf16[256,896]{1,0:T(8,128)(2,1)} %collective-permute-done.18.refs_2_), channel_id=1, source_target_pairs={{32,0},{48,16},{64,32},{80,48},{96,64},{112,80},{128,96},{144,112}... | collective-permute-start | bytes 1376264 | tf_op jit(solution)/shard_map/ppermute | solution.py:25
  107.6 25.8 %collective-permute-start.11 = (bf16[896,256]{1,0:T(8,128)(2,1)}, bf16[896,256]{1,0:T(8,128)(2,1)}, u32[]{:S(2)}, u32[]{:S(2)}) collective-permute-start(bf16[896,256]{1,0:T(8,128)(2,1)} %collective-permute-done.5.refs_4_.refs_8_), channel_id=1, source_target_pairs={{32,0},{48,16},{64,32},{80,48},{96,64},{112,80},{128,96},{144,112}... | collective-permute-start | bytes 1376264 | tf_op jit(solution)/shard_map/ppermute | solution.py:25
  114.0 23.2 %collective-permute-start.13 = (bf16[896,256]{1,0:T(8,128)(2,1)}, bf16[896,256]{1,0:T(8,128)(2,1)}, u32[]{:S(2)}, u32[]{:S(2)}) collective-permute-start(bf16[896,256]{1,0:T(8,128)(2,1)} %collective-permute-done.8.refs_3_.refs_7_), channel_id=1, source_target_pairs={{224,0},{240,16},{0,32},{16,48},{32,64},{48,80},{64,96},{80,112},{... | collective-permute-start | bytes 1376264 | tf_op jit(solution)/shard_map/ppermute | solution.py:25
  114.0 24.7 %collective-permute-start.12 = (bf16[896,256]{1,0:T(8,128)(2,1)}, bf16[896,256]{1,0:T(8,128)(2,1)}, u32[]{:S(2)}, u32[]{:S(2)}) collective-permute-start(bf16[896,256]{1,0:T(8,128)(2,1)} %collective-permute-done.10.refs_0_.refs_10_), channel_id=1, source_target_pairs={{224,0},{240,16},{0,32},{16,48},{32,64},{48,80},{64,96},{80,112},{... | collective-permute-start | bytes 1376264 | tf_op jit(solution)/shard_map/ppermute | solution.py:25
  115.5 27.7 %collective-permute-start.15 = (bf16[896,256]{1,0:T(8,128)(2,1)}, bf16[896,256]{1,0:T(8,128)(2,1)}, u32[]{:S(2)}, u32[]{:S(2)}) collective-permute-start(bf16[896,256]{1,0:T(8,128)(2,1)} %collective-permute-done.14.refs_4_.refs_13_), channel_id=1, source_target_pairs={{32,0},{48,16},{64,32},{80,48},{96,64},{112,80},{128,96},{144,112}... | collective-permute-start | bytes 1376264 | tf_op jit(solution)/shard_map/ppermute | solution.py:25
  127.2 20.2 %collective-permute-start.19 = (bf16[256,896]{1,0:T(8,128)(2,1)S(1)}, bf16[256,896]{1,0:T(8,128)(2,1)S(1)}, u32[]{:S(2)}, u32[]{:S(2)}) collective-permute-start(bf16[256,896]{1,0:T(8,128)(2,1)S(1)} %copy-done.13), channel_id=1, source_target_pairs={{224,0},{240,16},{0,32},{16,48},{32,64},{48,80},{64,96},{80,112},{... | collective-permute-start | bytes 1376264 | tf_op jit(solution)/shard_map/ppermute | solution.py:25
  133.4 19.2 %collective-permute-start.22 = (bf16[256,896]{1,0:T(8,128)(2,1)}, bf16[256,896]{1,0:T(8,128)(2,1)S(1)}, u32[]{:S(2)}, u32[]{:S(2)}) collective-permute-start(bf16[256,896]{1,0:T(8,128)(2,1)} %collective-permute-done.20.refs_4_), channel_id=1, source_target_pairs={{32,0},{48,16},{64,32},{80,48},{96,64},{112,80},{128,96},{144,112}... | collective-permute-start | bytes 1376264 | tf_op jit(solution)/shard_map/ppermute | solution.py:25
  147.1 18.7 %collective-permute-start.16 = (bf16[2,256,896]{2,1,0:T(8,128)(2,1)S(1)}, bf16[2,256,896]{2,1,0:T(8,128)(2,1)S(1)}, u32[]{:S(2)}, u32[]{:S(2)}) collective-permute-start(bf16[2,256,896]{2,1,0:T(8,128)(2,1)S(1)} %get-tuple-element.20), channel_id=1, source_target_pairs={{0,16},{16,0},{32,48},{48,32},{64,80},{80,64},{96,112},{112,96},{1... | collective-permute-start | bytes 2752520 | tf_op jit(solution)/shard_map/ppermute | solution.py:29
  173.9 21.2 %all-to-all-start.1 = ((bf16[16,128,256]{2,1,0:T(8,128)(2,1)}), bf16[16,128,256]{2,1,0:T(8,128)(2,1)S(1)}, u32[]{:S(2)}, u32[]{:S(2)}) async-start(bf16[16,128,256]{2,1,0:T(8,128)(2,1)} %shard_map.102), calls=%async_computation.1 | async-start | bytes 2097152 | tf_op jit(solution)/shard_map/all_to_all | solution.py:306
  195.2 21.0 %all-to-all-start.2 = ((bf16[16,128,256]{2,1,0:T(8,128)(2,1)}), bf16[16,128,256]{2,1,0:T(8,128)(2,1)S(1)}, u32[]{:S(2)}, u32[]{:S(2)}) async-start(bf16[16,128,256]{2,1,0:T(8,128)(2,1)} %shard_map.106), calls=%async_computation.2 | async-start | bytes 2097152 | tf_op jit(solution)/shard_map/all_to_all | solution.py:306
  203.3 17.5 %collective-permute-start.25 = (bf16[8,16,256]{2,1,0:T(8,128)(2,1)S(1)}, bf16[8,16,256]{2,1,0:T(8,128)(2,1)S(1)}, u32[]{:S(2)}, u32[]{:S(2)}) collective-permute-start(bf16[8,16,256]{2,1,0:T(8,128)(2,1)S(1)} %get-tuple-element.28), channel_id=1, source_target_pairs={{128,0},{144,16},{160,32},{176,48},{192,64},{208,80},{224,96},{240... | collective-permute-start | bytes 196616 | tf_op jit(solution)/shard_map/ppermute | solution.py:34
  (24 other events, 437.3 us)

commit v4 on v3

--- a/solution.py
+++ b/solution.py
@@ -115,7 +115,7 @@
 
 
 def gate_up_late(table, x, gate_early, up_early, *refs):
-    weights, (out, give, held, sems) = refs[:-4], refs[-4:]
+    weights, (out, held, sems) = refs[:-3], refs[-3:]
     late = RING - EARLY
     fetch(weights, held, sems)
     loop(2 * late, lambda i: fetched(held, sems, i))
@@ -123,9 +123,7 @@
     def tile(part):
         for which, early in enumerate((gate_early, up_early)):
             more = sum(dot_t(x[EARLY + n], held[which * late + n, part, :]) for n in range(late))
-            total = early[:, part] + more
-            out[which, :, part] = total
-            give[which, :, part] = total.astype(BF16)
+            out[which, :, part] = early[:, part] + more
 
     tile_loop(out.shape[2], tile)
 
@@ -158,8 +156,8 @@
 
 def outputs_kernel(table, mine, other, early, late, far, keep, give, hidden, both):
     def tile(part):
-        gate_pre = mine[0, :, part] + other[0, :, part].astype(F32)
-        up_pre = mine[1, :, part] + other[1, :, part].astype(F32)
+        gate_pre = mine[0, :, part] + other[0, :, part]
+        up_pre = mine[1, :, part] + other[1, :, part]
         activated = gate_pre * jax.nn.sigmoid(gate_pre)
         hidden[:, part] = (activated * up_pre).astype(BF16)
 
@@ -284,13 +282,13 @@
     gate_early = early_of(x_all, gate_all, True)[0]
     up_early = early_of(x_all, up_all, True)[0]
     late = RING - EARLY
-    parts, parts_give = call(
-        gate_up_late, [((2,) + by_row, F32), ((2,) + by_row, BF16)], table, x_all, gate_early, up_early,
+    parts = call(
+        gate_up_late, [((2,) + by_row, F32)], table, x_all, gate_early, up_early,
         loaded=gate_all[EARLY:] + up_all[EARLY:],
         scratch=[pltpu.VMEM((2 * late, ff, columns), BF16)] + arrivals(2 * late),
-    )
-    parts_other = swap(parts_give)
-    sums = parts + parts_other.astype(F32)
+    )[0]
+    parts_other = swap(parts)
+    sums = parts + parts_other
     gate_pre, up_pre = sums[0], sums[1]
     sigmoid_gate = jax.nn.sigmoid(gate_pre)
     activated = gate_pre * sigmoid_gate

time: 228 us -> 238 us (1.044)
  waiting for transfers between devices: 74.1 us -> 81.3 us
  local copies, waits for them, and re-layouts: 9.51 us -> 15.3 us
    unnamed x37 -> x47, local copies, waits for them, and re-layouts: 6.05 us -> 11.8 us
    ppermute x3, starting transfers between devices: 14.7 us -> 11.1 us  [opposite(): return lax.ppermute(block, 'dp', [((d + n // 2) % n, d) for d in range(n)])]
    all_to_all x2, waiting for transfers between devices: 12.2 us -> 15.6 us  [reduce_columns(): return lax.all_to_all(blocks_for, 'tensor', 0, 0, tiled=True)]
    ppermute x5, waiting for transfers between devices: 1.91 us -> 4.43 us  [swap(): return lax.ppermute(block, 'dp', [(d, d ^ 1) for d in range(2 * RING)])]
    ppermute x21, starting transfers between devices: 37.7 us -> 40.1 us  [ring(): return lax.ppermute(block, 'dp', route)]
  transfers between devices with their start and end apart: 31 -> 31, of which waited for: 17 -> 21; matrix products, arithmetic and copies ran while one was open for 4% -> 3% of each run, Pallas kernels for 15% -> 12%
where the time goes in v4:
time: 238 us; the launch traced here: 237 us
  waiting for transfers between devices  81.3 us (34%)
  starting transfers between devices  62.2 us (26%)
  Pallas kernels  35.7 us (15%)
  blocking collectives  34.1 us (14%)
  local copies, waits for them, and re-layouts  15.3 us (6%)
  other arithmetic  5.07 us (2%)
  between operations  3.1 us (1%)
    ppermute x21, waiting for transfers between devices, ring(): return lax.ppermute(block, 'dp', route)  54.9 us
    ppermute x21, starting transfers between devices, ring(): return lax.ppermute(block, 'dp', route)  40.1 us
    pallas_call x13, Pallas kernels, call(): pl.pallas_call(body, out_shape=[jax.ShapeDtypeStruct(s, d) for s, d in ou...  35.7 us
    all_to_all x1, blocking collectives, per_device(): every = lax.all_to_all(spread, 'tensor', 0, 0, tiled=True)  34.1 us
    all_to_all x2, waiting for transfers between devices, reduce_columns(): return lax.all_to_all(blocks_for, 'tensor', 0, 0, tiled=True)  15.6 us
    unnamed x47, local copies, waits for them, and re-layouts  11.8 us
    ppermute x3, starting transfers between devices, opposite(): return lax.ppermute(block, 'dp', [((d + n // 2) % n, d) for d in range(n)])  11.1 us
    all_to_all x2, starting transfers between devices, reduce_columns(): return lax.all_to_all(blocks_for, 'tensor', 0, 0, tiled=True)  10.4 us
  transfers between devices with their start and end apart: 31, of which 21 were waited for; matrix products, arithmetic and copies ran while one was open for 3% of the time, Pallas kernels for 12%

profile of v4, /device:TPU:2, one launch (start us, length us, event | category | flops | bytes accessed | tf_op | source)
XLA Modules:
  0.0 236.8 jit_solution(10176566826457696593)
XLA Ops:
  1.6 7.3 %collective-permute-start = (bf16[2,128,256]{2,1,0:T(8,128)(2,1)S(1)}, bf16[2,128,256]{2,1,0:T(8,128)(2,1)S(1)}, u32[]{:S(2)}, u32[]{:S(2)}) collective-permute-start(bf16[2,128,256]{2,1,0:T(8,128)(2,1)S(1)} %pad_maximum_fusion.1), channel_id=1, source_target_pairs={{128,0},{144,16},{160,32},{176,48},{192,64},{208,80},{224,96},{240... | collective-permute-start | bytes 393224 | tf_op jit(solution)/shard_map/ppermute | solution.py:34
  14.2 34.1 %all_to_all.15.mine = bf16[16,2,128,256]{3,2,1,0:T(8,128)(2,1)S(1)} all-to-all(bf16[16,2,128,256]{3,2,1,0:T(8,128)(2,1)S(1)} %broadcast_in_dim.71), channel_id=1, replica_groups=mesh['dp'=16,'tensor'=16] {'tensor'}, dimensions={0} | all-to-all | bytes 4194304 | tf_op jit(solution)/shard_map/all_to_all | solution.py:258
  49.3 4.9 %collective-permute-start.18 = (bf16[256,896]{1,0:T(8,128)(2,1)}, bf16[256,896]{1,0:T(8,128)(2,1)}, u32[]{:S(2)}, u32[]{:S(2)}) collective-permute-start(bf16[256,896]{1,0:T(8,128)(2,1)} %bitcast.13.refs_0_), channel_id=1, source_target_pairs={{32,0},{48,16},{64,32},{80,48},{96,64},{112,80},{128,96},{144,112}... | collective-permute-start | bytes 1376264 | tf_op jit(solution)/shard_map/ppermute | solution.py:25
  58.0 7.4 %collective-permute-done.18.refs_2_ = bf16[256,896]{1,0:T(8,128)(2,1)} collective-permute-done((bf16[256,896]{1,0:T(8,128)(2,1)}, bf16[256,896]{1,0:T(8,128)(2,1)}, u32[]{:S(2)}, u32[]{:S(2)}) %collective-permute-start.18) | collective-permute-done | bytes 458784 | tf_op jit(solution)/shard_map/ppermute | solution.py:25
  65.5 3.7 %collective-permute-start.3 = (bf16[896,256]{1,0:T(8,128)(2,1)S(1)}, bf16[896,256]{1,0:T(8,128)(2,1)S(1)}, u32[]{:S(2)}, u32[]{:S(2)}) collective-permute-start(bf16[896,256]{1,0:T(8,128)(2,1)S(1)} %bitcast.39), channel_id=1, source_target_pairs={{32,0},{48,16},{64,32},{80,48},{96,64},{112,80},{128,96},{144,112}... | collective-permute-start | bytes 1376264 | tf_op jit(solution)/shard_map/ppermute | solution.py:25
  69.2 6.0 %collective-permute-done.7.refs_2_.refs_5_ = bf16[896,256]{1,0:T(8,128)(2,1)S(1)} collective-permute-done((bf16[896,256]{1,0:T(8,128)(2,1)S(1)}, bf16[896,256]{1,0:T(8,128)(2,1)S(1)}, u32[]{:S(2)}, u32[]{:S(2)}) %collective-permute-start.7) | collective-permute-done | bytes 458784 | tf_op jit(solution)/shard_map/ppermute | solution.py:25
  75.2 3.7 %collective-permute-start.9 = (bf16[896,256]{1,0:T(8,128)(2,1)S(1)}, bf16[896,256]{1,0:T(8,128)(2,1)S(1)}, u32[]{:S(2)}, u32[]{:S(2)}) collective-permute-start(bf16[896,256]{1,0:T(8,128)(2,1)S(1)} %collective-permute-done.7.refs_2_.refs_5_), channel_id=1, source_target_pairs={{32,0},{48,16},{64,32},{80,48},{96,64},{112,80},{128,96},{144,112}... | collective-permute-start | bytes 1376264 | tf_op jit(solution)/shard_map/ppermute | solution.py:25
  85.0 3.7 %collective-permute-start.5 = (bf16[896,256]{1,0:T(8,128)(2,1)S(1)}, bf16[896,256]{1,0:T(8,128)(2,1)}, u32[]{:S(2)}, u32[]{:S(2)}) collective-permute-start(bf16[896,256]{1,0:T(8,128)(2,1)S(1)} %collective-permute-done.3.refs_2_.refs_4_), channel_id=1, source_target_pairs={{32,0},{48,16},{64,32},{80,48},{96,64},{112,80},{128,96},{144,112}... | collective-permute-start | bytes 1376264 | tf_op jit(solution)/shard_map/ppermute | solution.py:25
  89.5 5.3 %collective-permute-done.9.refs_4_.refs_9_ = bf16[896,256]{1,0:T(8,128)(2,1)S(1)} collective-permute-done((bf16[896,256]{1,0:T(8,128)(2,1)S(1)}, bf16[896,256]{1,0:T(8,128)(2,1)S(1)}, u32[]{:S(2)}, u32[]{:S(2)}) %collective-permute-start.9) | collective-permute-done | bytes 458784 | tf_op jit(solution)/shard_map/ppermute | solution.py:25
  94.8 3.7 %collective-permute-start.14 = (bf16[896,256]{1,0:T(8,128)(2,1)S(1)}, bf16[896,256]{1,0:T(8,128)(2,1)}, u32[]{:S(2)}, u32[]{:S(2)}) collective-permute-start(bf16[896,256]{1,0:T(8,128)(2,1)S(1)} %collective-permute-done.9.refs_4_.refs_9_), channel_id=1, source_target_pairs={{32,0},{48,16},{64,32},{80,48},{96,64},{112,80},{128,96},{144,112}... | collective-permute-start | bytes 1376264 | tf_op jit(solution)/shard_map/ppermute | solution.py:25
  104.7 3.8 %collective-permute-start.11 = (bf16[896,256]{1,0:T(8,128)(2,1)}, bf16[896,256]{1,0:T(8,128)(2,1)}, u32[]{:S(2)}, u32[]{:S(2)}) collective-permute-start(bf16[896,256]{1,0:T(8,128)(2,1)} %collective-permute-done.5.refs_4_.refs_8_), channel_id=1, source_target_pairs={{32,0},{48,16},{64,32},{80,48},{96,64},{112,80},{128,96},{144,112}... | collective-permute-start | bytes 1376264 | tf_op jit(solution)/shard_map/ppermute | solution.py:25
  108.5 6.0 %collective-permute-done.14.refs_4_.refs_13_ = bf16[896,256]{1,0:T(8,128)(2,1)} collective-permute-done((bf16[896,256]{1,0:T(8,128)(2,1)S(1)}, bf16[896,256]{1,0:T(8,128)(2,1)}, u32[]{:S(2)}, u32[]{:S(2)}) %collective-permute-start.14) | collective-permute-done | bytes 458784 | tf_op jit(solution)/shard_map/ppermute | solution.py:25
  114.5 3.8 %collective-permute-start.15 = (bf16[896,256]{1,0:T(8,128)(2,1)}, bf16[896,256]{1,0:T(8,128)(2,1)}, u32[]{:S(2)}, u32[]{:S(2)}) collective-permute-start(bf16[896,256]{1,0:T(8,128)(2,1)} %collective-permute-done.14.refs_4_.refs_13_), channel_id=1, source_target_pairs={{32,0},{48,16},{64,32},{80,48},{96,64},{112,80},{128,96},{144,112}... | collective-permute-start | bytes 1376264 | tf_op jit(solution)/shard_map/ppermute | solution.py:25
  118.3 3.9 %collective-permute-done.13.refs_3_.refs_11_ = bf16[896,256]{1,0:T(8,128)(2,1)} collective-permute-done((bf16[896,256]{1,0:T(8,128)(2,1)}, bf16[896,256]{1,0:T(8,128)(2,1)}, u32[]{:S(2)}, u32[]{:S(2)}) %collective-permute-start.13) | collective-permute-done | bytes 458784 | tf_op jit(solution)/shard_map/ppermute | solution.py:25
  127.6 3.9 %shard_map.97.up_early = f32[256,896]{1,0:T(8,128)S(1)} custom-call(s32[17]{0:T(128)S(1)} %pad_add_fusion.1.table, bf16[8,256,256]{2,1,0:T(8,128)(2,1)S(1)} %get-tuple-element.16.x, bf16[896,256]{1,0:T(8,128)(2,1)S(1)} %bitcast.36, bf16[896,256]{1,0:T(8,128)(2,1)S(1)} %copy-done.7, bf16[896,256]{1,0:T(8,128)(2,1)S(1)} %collective-permute-done.7.refs_2_.refs_5_, ...), custom_call_target="tpu_custom_call" | custom-call | tf_op jit(solution)/shard_map/pallas_call | solution.py:54
  131.5 4.1 %shard_map.96.gate_early = f32[256,896]{1,0:T(8,128)S(1)} custom-call(s32[17]{0:T(128)S(1)} %pad_add_fusion.1.table, bf16[8,256,256]{2,1,0:T(8,128)(2,1)S(1)} %get-tuple-element.16.x, bf16[896,256]{1,0:T(8,128)(2,1)S(1)} %bitcast.40, bf16[896,256]{1,0:T(8,128)(2,1)S(1)} %copy-done.5, bf16[896,256]{1,0:T(8,128)(2,1)S(1)} %copy-done.9, ...), custom_call_target="tpu_custom_call" | custom-call | tf_op jit(solution)/shard_map/pallas_call | solution.py:54
  135.7 3.9 %shard_map.98.mine = f32[2,256,896]{2,1,0:T(8,128)S(1)} custom-call(s32[17]{0:T(128)S(1)} %pad_add_fusion.1.table, bf16[8,256,256]{2,1,0:T(8,128)(2,1)S(1)} %get-tuple-element.16.x, f32[256,896]{1,0:T(8,128)S(1)} %shard_map.96.gate_early, f32[256,896]{1,0:T(8,128)S(1)} %shard_map.97.up_early, bf16[896,256]{1,0:T(8,128)(2,1)} %collective-permute-done.10.refs_0_.refs_10_, ...), custom_call_target="tpu_custom_call" | custom-call | tf_op jit(solution)/shard_map/pallas_call | solution.py:54
  147.3 6.7 %collective-permute-done.19.refs_3_ = bf16[256,896]{1,0:T(8,128)(2,1)S(1)} collective-permute-done((bf16[256,896]{1,0:T(8,128)(2,1)}, bf16[256,896]{1,0:T(8,128)(2,1)S(1)}, u32[]{:S(2)}, u32[]{:S(2)}) %collective-permute-start.19) | collective-permute-done | bytes 458784 | tf_op jit(solution)/shard_map/ppermute | solution.py:25
  173.4 6.7 %shard_map.105 = (bf16[8,128,256]{2,1,0:T(8,128)(2,1)S(1)}, bf16[8,128,256]{2,1,0:T(8,128)(2,1)S(1)}) custom-call(s32[17]{0:T(128)S(1)} %pad_add_fusion.1.table, f32[256,896]{1,0:T(8,128)S(1)} %shard_map.104.mine, f32[256,896]{1,0:T(8,128)S(1)} %collective-permute-done.26.other, f32[256,896]{1,0:T(8,128)S(1)} %get-tuple-element.33.by_gate, ...), custom_call_target="tpu_custom_call" | custom-call | tf_op jit(solution)/shard_map/pallas_call | solution.py:54
  183.8 4.9 %all-to-all-start.2 = ((bf16[16,128,256]{2,1,0:T(8,128)(2,1)}), bf16[16,128,256]{2,1,0:T(8,128)(2,1)S(1)}, u32[]{:S(2)}, u32[]{:S(2)}) async-start(bf16[16,128,256]{2,1,0:T(8,128)(2,1)} %shard_map.106), calls=%async_computation.2 | async-start | bytes 2097152 | tf_op jit(solution)/shard_map/all_to_all | solution.py:304
  200.3 4.9 %all-to-all-done.2.got = bf16[16,128,256]{2,1,0:T(8,128)(2,1)S(1)} async-done(((bf16[16,128,256]{2,1,0:T(8,128)(2,1)}), bf16[16,128,256]{2,1,0:T(8,128)(2,1)S(1)}, u32[]{:S(2)}, u32[]{:S(2)}) %all-to-all-start.2) | async-done | bytes 1048608 | tf_op jit(solution)/shard_map/all_to_all | solution.py:304
  205.2 5.5 %all-to-all-start.1 = ((bf16[16,128,256]{2,1,0:T(8,128)(2,1)}), bf16[16,128,256]{2,1,0:T(8,128)(2,1)S(1)}, u32[]{:S(2)}, u32[]{:S(2)}) async-start(bf16[16,128,256]{2,1,0:T(8,128)(2,1)} %shard_map.102), calls=%async_computation.1 | async-start | bytes 2097152 | tf_op jit(solution)/shard_map/all_to_all | solution.py:304
  215.5 10.8 %all-to-all-done.1.got = bf16[16,128,256]{2,1,0:T(8,128)(2,1)S(1)} async-done(((bf16[16,128,256]{2,1,0:T(8,128)(2,1)}), bf16[16,128,256]{2,1,0:T(8,128)(2,1)S(1)}, u32[]{:S(2)}, u32[]{:S(2)}) %all-to-all-start.1) | async-done | bytes 1048608 | tf_op jit(solution)/shard_map/all_to_all | solution.py:304
  229.1 6.3 %collective-permute-done.25 = bf16[8,16,256]{2,1,0:T(8,128)(2,1)S(1)} collective-permute-done((bf16[8,16,256]{2,1,0:T(8,128)(2,1)S(1)}, bf16[8,16,256]{2,1,0:T(8,128)(2,1)S(1)}, u32[]{:S(2)}, u32[]{:S(2)}) %collective-permute-start.25) | collective-permute-done | bytes 65568 | tf_op jit(solution)/shard_map/ppermute | solution.py:34
  (128 shorter events, 78.7 us)
Async XLA Ops:
  48.3 73.9 %collective-permute-start.1 = (bf16[16,2,128,256]{3,2,1,0:T(8,128)(2,1)S(1)}, bf16[16,2,128,256]{3,2,1,0:T(8,128)(2,1)}, u32[]{:S(2)}, u32[]{:S(2)}) collective-permute-start(bf16[16,2,128,256]{3,2,1,0:T(8,128)(2,1)S(1)} %all_to_all.15.mine), channel_id=1, source_target_pairs={{0,16},{16,0},{32,48},{48,32},{64,80},{80,64},{96,112},{112,96},{1... | collective-permute-start | bytes 6291464 | tf_op jit(solution)/shard_map/ppermute | solution.py:29
  49.3 16.1 %collective-permute-start.18 = (bf16[256,896]{1,0:T(8,128)(2,1)}, bf16[256,896]{1,0:T(8,128)(2,1)}, u32[]{:S(2)}, u32[]{:S(2)}) collective-permute-start(bf16[256,896]{1,0:T(8,128)(2,1)} %bitcast.13.refs_0_), channel_id=1, source_target_pairs={{32,0},{48,16},{64,32},{80,48},{96,64},{112,80},{128,96},{144,112}... | collective-permute-start | bytes 1376264 | tf_op jit(solution)/shard_map/ppermute | solution.py:25
  54.4 20.7 %collective-permute-start.7 = (bf16[896,256]{1,0:T(8,128)(2,1)S(1)}, bf16[896,256]{1,0:T(8,128)(2,1)S(1)}, u32[]{:S(2)}, u32[]{:S(2)}) collective-permute-start(bf16[896,256]{1,0:T(8,128)(2,1)S(1)} %bitcast.34), channel_id=1, source_target_pairs={{32,0},{48,16},{64,32},{80,48},{96,64},{112,80},{128,96},{144,112}... | collective-permute-start | bytes 1376264 | tf_op jit(solution)/shard_map/ppermute | solution.py:25
  57.9 21.0 %collective-permute-start.2 = (bf16[896,256]{1,0:T(8,128)(2,1)S(1)}, bf16[896,256]{1,0:T(8,128)(2,1)S(1)}, u32[]{:S(2)}, u32[]{:S(2)}) collective-permute-start(bf16[896,256]{1,0:T(8,128)(2,1)S(1)} %bitcast.38), channel_id=1, source_target_pairs={{224,0},{240,16},{0,32},{16,48},{32,64},{48,80},{64,96},{80,112},{... | collective-permute-start | bytes 1376264 | tf_op jit(solution)/shard_map/ppermute | solution.py:25
  58.0 23.4 %collective-permute-start.6 = (bf16[896,256]{1,0:T(8,128)(2,1)S(1)}, bf16[896,256]{1,0:T(8,128)(2,1)S(1)}, u32[]{:S(2)}, u32[]{:S(2)}) collective-permute-start(bf16[896,256]{1,0:T(8,128)(2,1)S(1)} %bitcast.35), channel_id=1, source_target_pairs={{224,0},{240,16},{0,32},{16,48},{32,64},{48,80},{64,96},{80,112},{... | collective-permute-start | bytes 1376264 | tf_op jit(solution)/shard_map/ppermute | solution.py:25
  65.5 19.6 %collective-permute-start.3 = (bf16[896,256]{1,0:T(8,128)(2,1)S(1)}, bf16[896,256]{1,0:T(8,128)(2,1)S(1)}, u32[]{:S(2)}, u32[]{:S(2)}) collective-permute-start(bf16[896,256]{1,0:T(8,128)(2,1)S(1)} %bitcast.39), channel_id=1, source_target_pairs={{32,0},{48,16},{64,32},{80,48},{96,64},{112,80},{128,96},{144,112}... | collective-permute-start | bytes 1376264 | tf_op jit(solution)/shard_map/ppermute | solution.py:25
  75.2 19.7 %collective-permute-start.9 = (bf16[896,256]{1,0:T(8,128)(2,1)S(1)}, bf16[896,256]{1,0:T(8,128)(2,1)S(1)}, u32[]{:S(2)}, u32[]{:S(2)}) collective-permute-start(bf16[896,256]{1,0:T(8,128)(2,1)S(1)} %collective-permute-done.7.refs_2_.refs_5_), channel_id=1, source_target_pairs={{32,0},{48,16},{64,32},{80,48},{96,64},{112,80},{128,96},{144,112}... | collective-permute-start | bytes 1376264 | tf_op jit(solution)/shard_map/ppermute | solution.py:25
  78.9 20.4 %collective-permute-start.4 = (bf16[896,256]{1,0:T(8,128)(2,1)S(1)}, bf16[896,256]{1,0:T(8,128)(2,1)S(1)}, u32[]{:S(2)}, u32[]{:S(2)}) collective-permute-start(bf16[896,256]{1,0:T(8,128)(2,1)S(1)} %collective-permute-done.2.refs_1_.refs_2_), channel_id=1, source_target_pairs={{224,0},{240,16},{0,32},{16,48},{32,64},{48,80},{64,96},{80,112},{... | collective-permute-start | bytes 1376264 | tf_op jit(solution)/shard_map/ppermute | solution.py:25
  81.3 20.0 %collective-permute-start.8 = (bf16[896,256]{1,0:T(8,128)(2,1)S(1)}, bf16[896,256]{1,0:T(8,128)(2,1)}, u32[]{:S(2)}, u32[]{:S(2)}) collective-permute-start(bf16[896,256]{1,0:T(8,128)(2,1)S(1)} %collective-permute-done.6.refs_1_.refs_3_), channel_id=1, source_target_pairs={{224,0},{240,16},{0,32},{16,48},{32,64},{48,80},{64,96},{80,112},{... | collective-permute-start | bytes 1376264 | tf_op jit(solution)/shard_map/ppermute | solution.py:25
  85.0 19.7 %collective-permute-start.5 = (bf16[896,256]{1,0:T(8,128)(2,1)S(1)}, bf16[896,256]{1,0:T(8,128)(2,1)}, u32[]{:S(2)}, u32[]{:S(2)}) collective-permute-start(bf16[896,256]{1,0:T(8,128)(2,1)S(1)} %collective-permute-done.3.refs_2_.refs_4_), channel_id=1, source_target_pairs={{32,0},{48,16},{64,32},{80,48},{96,64},{112,80},{128,96},{144,112}... | collective-permute-start | bytes 1376264 | tf_op jit(solution)/shard_map/ppermute | solution.py:25
  94.8 19.7 %collective-permute-start.14 = (bf16[896,256]{1,0:T(8,128)(2,1)S(1)}, bf16[896,256]{1,0:T(8,128)(2,1)}, u32[]{:S(2)}, u32[]{:S(2)}) collective-permute-start(bf16[896,256]{1,0:T(8,128)(2,1)S(1)} %collective-permute-done.9.refs_4_.refs_9_), channel_id=1, source_target_pairs={{32,0},{48,16},{64,32},{80,48},{96,64},{112,80},{128,96},{144,112}... | collective-permute-start | bytes 1376264 | tf_op jit(solution)/shard_map/ppermute | solution.py:25
  99.3 19.0 %collective-permute-start.10 = (bf16[896,256]{1,0:T(8,128)(2,1)S(1)}, bf16[896,256]{1,0:T(8,128)(2,1)}, u32[]{:S(2)}, u32[]{:S(2)}) collective-permute-start(bf16[896,256]{1,0:T(8,128)(2,1)S(1)} %collective-permute-done.4.refs_3_.refs_6_), channel_id=1, source_target_pairs={{224,0},{240,16},{0,32},{16,48},{32,64},{48,80},{64,96},{80,112},{... | collective-permute-start | bytes 1376264 | tf_op jit(solution)/shard_map/ppermute | solution.py:25
  101.3 20.9 %collective-permute-start.13 = (bf16[896,256]{1,0:T(8,128)(2,1)}, bf16[896,256]{1,0:T(8,128)(2,1)}, u32[]{:S(2)}, u32[]{:S(2)}) collective-permute-start(bf16[896,256]{1,0:T(8,128)(2,1)} %collective-permute-done.8.refs_3_.refs_7_), channel_id=1, source_target_pairs={{224,0},{240,16},{0,32},{16,48},{32,64},{48,80},{64,96},{80,112},{... | collective-permute-start | bytes 1376264 | tf_op jit(solution)/shard_map/ppermute | solution.py:25
  104.7 31.0 %collective-permute-start.11 = (bf16[896,256]{1,0:T(8,128)(2,1)}, bf16[896,256]{1,0:T(8,128)(2,1)}, u32[]{:S(2)}, u32[]{:S(2)}) collective-permute-start(bf16[896,256]{1,0:T(8,128)(2,1)} %collective-permute-done.5.refs_4_.refs_8_), channel_id=1, source_target_pairs={{32,0},{48,16},{64,32},{80,48},{96,64},{112,80},{128,96},{144,112}... | collective-permute-start | bytes 1376264 | tf_op jit(solution)/shard_map/ppermute | solution.py:25
  114.5 21.1 %collective-permute-start.15 = (bf16[896,256]{1,0:T(8,128)(2,1)}, bf16[896,256]{1,0:T(8,128)(2,1)}, u32[]{:S(2)}, u32[]{:S(2)}) collective-permute-start(bf16[896,256]{1,0:T(8,128)(2,1)} %collective-permute-done.14.refs_4_.refs_13_), channel_id=1, source_target_pairs={{32,0},{48,16},{64,32},{80,48},{96,64},{112,80},{128,96},{144,112}... | collective-permute-start | bytes 1376264 | tf_op jit(solution)/shard_map/ppermute | solution.py:25
  118.3 17.4 %collective-permute-start.12 = (bf16[896,256]{1,0:T(8,128)(2,1)}, bf16[896,256]{1,0:T(8,128)(2,1)}, u32[]{:S(2)}, u32[]{:S(2)}) collective-permute-start(bf16[896,256]{1,0:T(8,128)(2,1)} %collective-permute-done.10.refs_0_.refs_10_), channel_id=1, source_target_pairs={{224,0},{240,16},{0,32},{16,48},{32,64},{48,80},{64,96},{80,112},{... | collective-permute-start | bytes 1376264 | tf_op jit(solution)/shard_map/ppermute | solution.py:25
  122.2 19.2 %collective-permute-start.17 = (bf16[256,896]{1,0:T(8,128)(2,1)}, bf16[256,896]{1,0:T(8,128)(2,1)}, u32[]{:S(2)}, u32[]{:S(2)}) collective-permute-start(bf16[256,896]{1,0:T(8,128)(2,1)} %bitcast.13.refs_0_), channel_id=1, source_target_pairs={{224,0},{240,16},{0,32},{16,48},{32,64},{48,80},{64,96},{80,112},{... | collective-permute-start | bytes 1376264 | tf_op jit(solution)/shard_map/ppermute | solution.py:25
  122.2 21.4 %collective-permute-start.20 = (bf16[256,896]{1,0:T(8,128)(2,1)}, bf16[256,896]{1,0:T(8,128)(2,1)}, u32[]{:S(2)}, u32[]{:S(2)}) collective-permute-start(bf16[256,896]{1,0:T(8,128)(2,1)} %collective-permute-done.18.refs_2_), channel_id=1, source_target_pairs={{32,0},{48,16},{64,32},{80,48},{96,64},{112,80},{128,96},{144,112}... | collective-permute-start | bytes 1376264 | tf_op jit(solution)/shard_map/ppermute | solution.py:25
  139.6 31.4 %collective-permute-start.16 = (f32[2,256,896]{2,1,0:T(8,128)S(1)}, f32[2,256,896]{2,1,0:T(8,128)S(1)}, u32[]{:S(2)}, u32[]{:S(2)}) collective-permute-start(f32[2,256,896]{2,1,0:T(8,128)S(1)} %shard_map.98.mine), channel_id=1, source_target_pairs={{0,16},{16,0},{32,48},{48,32},{64,80},{80,64},{96,112},{112,96},{1... | collective-permute-start | bytes 5505032 | tf_op jit(solution)/shard_map/ppermute | solution.py:29
  141.4 12.6 %collective-permute-start.19 = (bf16[256,896]{1,0:T(8,128)(2,1)}, bf16[256,896]{1,0:T(8,128)(2,1)S(1)}, u32[]{:S(2)}, u32[]{:S(2)}) collective-permute-start(bf16[256,896]{1,0:T(8,128)(2,1)} %collective-permute-done.17.refs_1_), channel_id=1, source_target_pairs={{224,0},{240,16},{0,32},{16,48},{32,64},{48,80},{64,96},{80,112},{... | collective-permute-start | bytes 1376264 | tf_op jit(solution)/shard_map/ppermute | solution.py:25
  143.6 13.6 %collective-permute-start.22 = (bf16[256,896]{1,0:T(8,128)(2,1)}, bf16[256,896]{1,0:T(8,128)(2,1)S(1)}, u32[]{:S(2)}, u32[]{:S(2)}) collective-permute-start(bf16[256,896]{1,0:T(8,128)(2,1)} %collective-permute-done.20.refs_4_), channel_id=1, source_target_pairs={{32,0},{48,16},{64,32},{80,48},{96,64},{112,80},{128,96},{144,112}... | collective-permute-start | bytes 1376264 | tf_op jit(solution)/shard_map/ppermute | solution.py:25
  183.8 21.4 %all-to-all-start.2 = ((bf16[16,128,256]{2,1,0:T(8,128)(2,1)}), bf16[16,128,256]{2,1,0:T(8,128)(2,1)S(1)}, u32[]{:S(2)}, u32[]{:S(2)}) async-start(bf16[16,128,256]{2,1,0:T(8,128)(2,1)} %shard_map.106), calls=%async_computation.2 | async-start | bytes 2097152 | tf_op jit(solution)/shard_map/all_to_all | solution.py:304
  205.2 21.1 %all-to-all-start.1 = ((bf16[16,128,256]{2,1,0:T(8,128)(2,1)}), bf16[16,128,256]{2,1,0:T(8,128)(2,1)S(1)}, u32[]{:S(2)}, u32[]{:S(2)}) async-start(bf16[16,128,256]{2,1,0:T(8,128)(2,1)} %shard_map.102), calls=%async_computation.1 | async-start | bytes 2097152 | tf_op jit(solution)/shard_map/all_to_all | solution.py:304
  213.6 15.5 %collective-permute-start.28 = (bf16[8,16,256]{2,1,0:T(8,128)(2,1)S(1)}, bf16[8,16,256]{2,1,0:T(8,128)(2,1)S(1)}, u32[]{:S(2)}, u32[]{:S(2)}) collective-permute-start(bf16[8,16,256]{2,1,0:T(8,128)(2,1)S(1)} %get-tuple-element.29), channel_id=1, source_target_pairs={{128,0},{144,16},{160,32},{176,48},{192,64},{208,80},{224,96},{240... | collective-permute-start | bytes 196616 | tf_op jit(solution)/shard_map/ppermute | solution.py:34
  (29 other events, 322.1 us)
